TPU v7x, 128 devices: a whole 4x4x4 slice. The times are simulated.
128 devices in a mesh: gossip: 32 (over z, y_lo, x), mp: 4 (over y_hi, core).
Axes of the slice: x: 4, y: 4 (y_hi: 2, y_lo: 2; y = y_hi * 2 + y_lo), z: 4, core: 2. Of those that a mesh axis runs over, the one named last changes fastest.
Arguments:
- tokens: bfloat16 [32, 512, 2048], P('gossip'), may hold values from -6 to 6
- targets: bfloat16 [32, 512, 2048], P('gossip'), may hold values from -6 to 6
- gate_weight: bfloat16 [32, 2048, 4096], P('gossip', None, 'mp'), may hold values from -6 to 6
- up_weight: bfloat16 [32, 2048, 4096], P('gossip', None, 'mp'), may hold values from -6 to 6
- down_weight: bfloat16 [32, 4096, 2048], P('gossip', 'mp'), may hold values from -6 to 6
Outputs:
- gate_out: bfloat16 [32, 2048, 4096], P('gossip', None, 'mp')
- up_out: bfloat16 [32, 2048, 4096], P('gossip', None, 'mp')
- down_out: bfloat16 [32, 4096, 2048], P('gossip', 'mp')
All inputs are finite; a program needn't handle non-finite values.
Results may differ from a plain program's by a relative error of at most 0.0095.
Values may be sent and summed in bfloat16 or wider, within the bound.
A program may use at most 128 MiB of HBM per device.

v0:
```python
import jax
import jax.numpy as jnp
from jax import lax
from jax.sharding import PartitionSpec as P

ITERS = 1


def passed_along(value, axis, steps):
    count = lax.axis_size(axis)
    pairs = [(source, (source + steps) % count) for source in range(count)]
    return lax.ppermute(value, axis, pairs)


def rms_norm(values):
    widened = values.astype(jnp.float32)
    return (
        widened * lax.rsqrt(jnp.mean(widened * widened, axis=-1, keepdims=True) + 1e-06)
    ).astype(jnp.bfloat16)


def mix_three(lower, own, upper):
    total = lower.astype(jnp.float32) + own.astype(jnp.float32) + upper.astype(jnp.float32)
    return (total / 3.0).astype(jnp.bfloat16)


def local(tokens, targets, gate_weight, up_weight, down_weight):
    inputs = tokens[0]
    wanted = targets[0]
    w_gate = gate_weight[0]
    w_up = up_weight[0]
    w_down = down_weight[0]
    tok_count = inputs.shape[0]
    width = inputs.shape[1]
    mp_count = lax.axis_size("mp")
    hidden_all = w_gate.shape[1] * mp_count
    in_scale = 1.0 / width**0.5
    mid_scale = 1.0 / hidden_all**0.5
    step_size = hidden_all / 4.0
    normed = rms_norm(inputs)
    offset = inputs.astype(jnp.float32) - wanted.astype(jnp.float32)
    own_rows = tok_count // mp_count
    offset_own = lax.dynamic_slice_in_dim(offset, lax.axis_index("mp") * own_rows, own_rows, 0)
    for iteration in range(ITERS):
        gate_pre = jnp.dot(normed, w_gate, preferred_element_type=jnp.float32) * in_scale
        up_pre = jnp.dot(normed, w_up, preferred_element_type=jnp.float32) * in_scale
        sig_gate = jax.nn.sigmoid(gate_pre)
        act_gate = gate_pre * sig_gate
        hidden = (act_gate * up_pre).astype(jnp.bfloat16)
        partial_value = jnp.dot(hidden, w_down, preferred_element_type=jnp.float32)
        output_own = (
            lax.psum_scatter(
                partial_value.astype(jnp.bfloat16), "mp", scatter_dimension=0, tiled=True
            ).astype(jnp.float32)
            * mid_scale
        )
        err_own = ((offset_own + output_own) / tok_count).astype(jnp.bfloat16)
        err_grad = lax.all_gather(err_own, "mp", axis=0, tiled=True)
        grad_down = (
            jnp.einsum("tf,td->fd", hidden, err_grad, preferred_element_type=jnp.float32)
            * mid_scale
        )
        new_down = (w_down.astype(jnp.float32) - step_size * grad_down).astype(jnp.bfloat16)
        down_low = passed_along(new_down, "gossip", 1)
        down_high = passed_along(new_down, "gossip", -1)
        grad_hidden = (
            jnp.einsum("td,fd->tf", err_grad, w_down, preferred_element_type=jnp.float32)
            * mid_scale
        )
        grad_gate = (
            grad_hidden * up_pre * (sig_gate * (1.0 + gate_pre * (1.0 - sig_gate)))
        ).astype(jnp.bfloat16)
        grad_up = (grad_hidden * act_gate).astype(jnp.bfloat16)
        grad_wgate = (
            jnp.einsum("td,tf->df", normed, grad_gate, preferred_element_type=jnp.float32)
            * in_scale
        )
        grad_wup = (
            jnp.einsum("td,tf->df", normed, grad_up, preferred_element_type=jnp.float32) * in_scale
        )
        new_gate = (w_gate.astype(jnp.float32) - step_size * grad_wgate).astype(jnp.bfloat16)
        new_up = (w_up.astype(jnp.float32) - step_size * grad_wup).astype(jnp.bfloat16)
        inner = jnp.stack([new_gate, new_up])
        inner_low = passed_along(inner, "gossip", 1)
        inner_high = passed_along(inner, "gossip", -1)
        inner_mixed = mix_three(inner_low, inner, inner_high)
        w_gate = inner_mixed[0]
        w_up = inner_mixed[1]
        w_down = mix_three(down_low, new_down, down_high)
    return (w_gate[None], w_up[None], w_down[None])


def solution(mesh):
    placed = (
        P("gossip", None, None),
        P("gossip", None, None),
        P("gossip", None, "mp"),
        P("gossip", None, "mp"),
        P("gossip", "mp", None),
    )
    return jax.shard_map(
        local,
        mesh=mesh,
        in_specs=placed,
        out_specs=(P("gossip", None, "mp"), P("gossip", None, "mp"), P("gossip", "mp", None)),
        check_vma=False,
    )
```

profile of v0, /device:TPU:1, one launch (start us, length us, event | category | flops | bytes accessed | tf_op | source)
XLA Modules:
  0.0 424.5 jit_solution(3292398702142443393)
XLA Ops:
  7.2 0.0 reduce-scatter.2.cloned.1.call-start
  7.2 2.1 multiply_reduce_fusion
  9.3 0.0 copy-start.4
  9.3 5.3 %fusion.8 = f32[512,1024]{1,0:T(8,128)S(1)} fusion(bf16[1,2048,1024]{2,1,0:T(8,128)(2,1)} %param.7, bf16[1,512,2048]{2,1,0:T(8,128)(2,1)} %param.5, f32[512]{0:T(512)S(1)} %add_rsqrt_fusion), kind=kOutput, calls=%fused_computation.16 | convolution fusion | flops 2150629376 | bytes 8390656 | tf_op jit(solution)/shard_map/dot_general | solution.py:45
  14.7 0.0 copy-start.7
  14.7 4.0 multiply_convert_fusion.5
  18.7 1.0 copy-done.11
  19.7 3.7 fusion.12
  23.4 0.0 reduce-scatter.2.cloned.1.call-update
  23.4 0.2 all-gather.2.cloned.1.call-start
  23.7 2.5 convert_bitcast_fusion
  26.2 38.3 %reduce-scatter.2.cloned.1.call-done = bf16[128,2048]{1,0:T(8,128)(2,1)} async-done(((bf16[512,2048]{1,0:T(8,128)(2,1)}), bf16[128,2048]{1,0:T(8,128)(2,1)}) %reduce-scatter.2.cloned.1.call-update) | async-done | bytes 524304 | tf_op jit(solution)/shard_map/reduce_scatter | solution.py:52
  64.5 2.5 fusion.19
  67.0 0.0 all-gather.2.cloned.1.call-update
  67.0 27.2 %all-gather.2.cloned.1.call-done = bf16[512,2048]{1,0:T(8,128)(2,1)} async-done(((bf16[128,2048]{1,0:T(8,128)(2,1)}), bf16[512,2048]{1,0:T(8,128)(2,1)}) %all-gather.2.cloned.1.call-update) | async-done | bytes 2097168 | tf_op jit(solution)/shard_map/all_gather | solution.py:58
  94.2 5.3 %fusion.2 = f32[512,1024]{1,0:T(8,128)S(1)} fusion(bf16[512,2048]{1,0:T(8,128)(2,1)} %all-gather.2.cloned.1.call-done, bf16[1,1024,2048]{2,1,0:T(8,128)(2,1)} %param.9), kind=kOutput, calls=%fused_computation.10 | convolution fusion | flops 2147483648 | bytes 8388608 | tf_op jit(solution)/shard_map/td,fd->tf/dot_general | solution.py:67
  99.5 0.0 copy-start.6
  99.6 0.0 copy-start.12
  99.6 3.1 fusion.11
  102.7 4.8 %fusion.10 = bf16[1,2048,1024]{2,1,0:T(8,128)(2,1)} fusion(bf16[1,2048,1024]{2,1,0:T(8,128)(2,1)S(1)} %copy-done.6, f32[512,1024]{1,0:T(8,128)S(1)} %fusion.2, f32[512,1024]{1,0:T(8,128)S(1)} %copy-done.12, f32[512,1024]{1,0:T(8,128)S(1)} %copy-done.10, bf16[1,512,2048]{2,1,0:T(8,128)(2,1)S(1)} %copy-done.1, f32[512]{0:T(512)S(1)} %add_rsqrt_fusion), kind=kOutput, calls=%fused_computation.20 | convolution fusion | flops 2165833728 | bytes 16779264 | tf_op jit(solution)/shard_map/td,tf->df/dot_general | solution.py:75
  107.5 6.3 %pad_maximum_fusion = bf16[2,2048,1024]{2,1,0:T(8,128)(2,1)} fusion(bf16[1,2048,1024]{2,1,0:T(8,128)(2,1)S(1)} %fusion.11, bf16[1,2048,1024]{2,1,0:T(8,128)(2,1)} %fusion.10), kind=kLoop, calls=%fused_computation.1 | loop fusion | flops 4194304 | bytes 16777216 | tf_op jit(solution)/shard_map/stack | solution.py:83
  113.8 4.8 %collective-permute-start.1 = (bf16[2,2048,1024]{2,1,0:T(8,128)(2,1)}, bf16[2,2048,1024]{2,1,0:T(8,128)(2,1)}, u32[]{:S(2)}, u32[]{:S(2)}) collective-permute-start(bf16[2,2048,1024]{2,1,0:T(8,128)(2,1)} %pad_maximum_fusion), channel_id=1, source_target_pairs={{0,124},{4,0},{8,4},{12,8},{16,12},{20,16},{24,20},{28,24},{32,28}... | collective-permute-start | bytes 25165832 | tf_op jit(solution)/shard_map/ppermute | solution.py:12
  118.7 5.0 %subtract_convert_fusion = bf16[1024,2048]{1,0:T(8,128)(2,1)S(1)} fusion(bf16[512,1024]{1,0:T(8,128)(2,1)} %copy-done.11, bf16[512,2048]{1,0:T(8,128)(2,1)S(1)} %copy-done.8, bf16[1,1024,2048]{2,1,0:T(8,128)(2,1)} %param.9), kind=kOutput, calls=%fused_computation.3 | convolution fusion | flops 2155872256 | bytes 11534336 | tf_op jit(solution)/shard_map/tf,td->fd/dot_general | solution.py:60
  123.7 0.0 copy-start.2
  123.7 0.0 copy-start
  123.8 5.7 %collective-permute-start.3 = (bf16[1024,2048]{1,0:T(8,128)(2,1)S(1)}, bf16[1024,2048]{1,0:T(8,128)(2,1)S(1)}, u32[]{:S(2)}, u32[]{:S(2)}) collective-permute-start(bf16[1024,2048]{1,0:T(8,128)(2,1)S(1)} %subtract_convert_fusion), channel_id=1, source_target_pairs={{0,124},{4,0},{8,4},{12,8},{16,12},{20,16},{24,20},{28,24},{32,28}... | collective-permute-start | bytes 12582920 | tf_op jit(solution)/shard_map/ppermute | solution.py:12
  129.5 258.8 %collective-permute-done.3 = bf16[1024,2048]{1,0:T(8,128)(2,1)S(1)} collective-permute-done((bf16[1024,2048]{1,0:T(8,128)(2,1)S(1)}, bf16[1024,2048]{1,0:T(8,128)(2,1)S(1)}, u32[]{:S(2)}, u32[]{:S(2)}) %collective-permute-start.3) | collective-permute-done | bytes 4194336 | tf_op jit(solution)/shard_map/ppermute | solution.py:12
  388.3 2.0 copy-done.3
  390.3 4.3 %collective-permute-done.2 = bf16[1024,2048]{1,0:T(8,128)(2,1)} collective-permute-done((bf16[1024,2048]{1,0:T(8,128)(2,1)S(1)}, bf16[1024,2048]{1,0:T(8,128)(2,1)}, u32[]{:S(2)}, u32[]{:S(2)}) %collective-permute-start.2) | collective-permute-done | bytes 4194336 | tf_op jit(solution)/shard_map/ppermute | solution.py:12
  394.5 10.1 %fusion.1 = bf16[1,1024,2048]{2,1,0:T(8,128)(2,1)} fusion(bf16[1024,2048]{1,0:T(8,128)(2,1)} %copy-done.3, bf16[1024,2048]{1,0:T(8,128)(2,1)} %copy-done.2, bf16[1024,2048]{1,0:T(8,128)(2,1)} %collective-permute-done.2), kind=kLoop, calls=%fused_computation.9 | loop fusion | flops 14680064 | bytes 16777216 | tf_op jit(solution)/shard_map/broadcast_in_dim | solution.py:90
  404.6 9.2 %multiply_convert_fusion = bf16[2,2048,1024]{2,1,0:T(8,128)(2,1)S(1)} fusion(bf16[2,2048,1024]{2,1,0:T(8,128)(2,1)} %collective-permute-done.1, bf16[2,2048,1024]{2,1,0:T(8,128)(2,1)} %collective-permute-done, bf16[1,2048,1024]{2,1,0:T(8,128)(2,1)S(1)} %fusion.11, bf16[1,2048,1024]{2,1,0:T(8,128)(2,1)S(1)} %copy-done), kind=kLoop, calls=%fused_computation | loop fusion | flops 33554432 | bytes 33554432 | tf_op jit(solution)/shard_map/convert_element_type | solution.py:24
  413.8 3.8 fusion.33
  (23 shorter events, 0.1 us)
Async XLA Ops:
  7.2 57.3 %reduce-scatter.2.cloned.1.call-start = ((), (), s32[]{:S(2)}) async-start(), calls=%async_computation.1 | async-start | bytes 2621440 | tf_op jit(solution)/shard_map/reduce_scatter | solution.py:52
  9.3 5.4 %copy-start.1 = (bf16[1,512,2048]{2,1,0:T(8,128)(2,1)S(1)}, bf16[1,512,2048]{2,1,0:T(8,128)(2,1)}, u32[]{:S(2)}) copy-start(bf16[1,512,2048]{2,1,0:T(8,128)(2,1)} %param.5) | copy-start | bytes 6291460
  9.3 5.4 %copy-start.4 = (bf16[1,2048,1024]{2,1,0:T(8,128)(2,1)S(1)}, bf16[1,2048,1024]{2,1,0:T(8,128)(2,1)}, u32[]{:S(2)}) copy-start(bf16[1,2048,1024]{2,1,0:T(8,128)(2,1)} %param.8) | copy-start | bytes 12582916
  14.7 4.1 copy-start.9
  14.7 5.0 %copy-start.7 = (bf16[1,1024,2048]{2,1,0:T(8,128)(2,1)S(1)}, bf16[1,1024,2048]{2,1,0:T(8,128)(2,1)}, u32[]{:S(2)}) copy-start(bf16[1,1024,2048]{2,1,0:T(8,128)(2,1)} %param.9) | copy-start | bytes 12582916
  18.7 1.0 copy-start.11
  23.4 70.8 %all-gather.2.cloned.1.call-start = ((), (), s32[]{:S(2)}) async-start(), calls=%async_computation.2 | async-start | bytes 2621440 | tf_op jit(solution)/shard_map/all_gather | solution.py:58
  94.2 5.3 %copy-start.5 = (bf16[1,2048,1024]{2,1,0:T(8,128)(2,1)S(1)}, bf16[1,2048,1024]{2,1,0:T(8,128)(2,1)}, u32[]{:S(2)}) copy-start(bf16[1,2048,1024]{2,1,0:T(8,128)(2,1)} %param.8) | copy-start | bytes 12582916
  94.2 5.3 %copy-start.10 = (f32[512,1024]{1,0:T(8,128)S(1)}, f32[512,1024]{1,0:T(8,128)}, u32[]{:S(2)}) copy-start(f32[512,1024]{1,0:T(8,128)} %copy-done.9) | copy-start | bytes 6291460
  99.5 3.1 copy-start.6
  99.6 3.1 copy-start.12
  107.5 11.2 %copy-start.8 = (bf16[512,2048]{1,0:T(8,128)(2,1)S(1)}, bf16[512,2048]{1,0:T(8,128)(2,1)}, u32[]{:S(2)}) copy-start(bf16[512,2048]{1,0:T(8,128)(2,1)} %all-gather.2.cloned.1.call-done) | copy-start | bytes 6291460
  113.8 290.8 %collective-permute-start.1 = (bf16[2,2048,1024]{2,1,0:T(8,128)(2,1)}, bf16[2,2048,1024]{2,1,0:T(8,128)(2,1)}, u32[]{:S(2)}, u32[]{:S(2)}) collective-permute-start(bf16[2,2048,1024]{2,1,0:T(8,128)(2,1)} %pad_maximum_fusion), channel_id=1, source_target_pairs={{0,124},{4,0},{8,4},{12,8},{16,12},{20,16},{24,20},{28,24},{32,28}... | collective-permute-start | bytes 25165832 | tf_op jit(solution)/shard_map/ppermute | solution.py:12
  118.7 286.0 %collective-permute-start = (bf16[2,2048,1024]{2,1,0:T(8,128)(2,1)}, bf16[2,2048,1024]{2,1,0:T(8,128)(2,1)}, u32[]{:S(2)}, u32[]{:S(2)}) collective-permute-start(bf16[2,2048,1024]{2,1,0:T(8,128)(2,1)} %pad_maximum_fusion), channel_id=1, source_target_pairs={{0,4},{4,8},{8,12},{12,16},{16,20},{20,24},{24,28},{28,32},{32,36}... | collective-permute-start | bytes 25165832 | tf_op jit(solution)/shard_map/ppermute | solution.py:12
  123.7 5.8 %copy-start.2 = (bf16[1024,2048]{1,0:T(8,128)(2,1)}, bf16[1024,2048]{1,0:T(8,128)(2,1)S(1)}, u32[]{:S(2)}) copy-start(bf16[1024,2048]{1,0:T(8,128)(2,1)S(1)} %subtract_convert_fusion) | copy-start | bytes 12582916
  123.7 280.9 %copy-start = (bf16[1,2048,1024]{2,1,0:T(8,128)(2,1)S(1)}, bf16[1,2048,1024]{2,1,0:T(8,128)(2,1)}, u32[]{:S(2)}) copy-start(bf16[1,2048,1024]{2,1,0:T(8,128)(2,1)} %fusion.10) | copy-start | bytes 12582916
  123.8 264.5 %collective-permute-start.3 = (bf16[1024,2048]{1,0:T(8,128)(2,1)S(1)}, bf16[1024,2048]{1,0:T(8,128)(2,1)S(1)}, u32[]{:S(2)}, u32[]{:S(2)}) collective-permute-start(bf16[1024,2048]{1,0:T(8,128)(2,1)S(1)} %subtract_convert_fusion), channel_id=1, source_target_pairs={{0,124},{4,0},{8,4},{12,8},{16,12},{20,16},{24,20},{28,24},{32,28}... | collective-permute-start | bytes 12582920 | tf_op jit(solution)/shard_map/ppermute | solution.py:12
  129.5 265.0 %collective-permute-start.2 = (bf16[1024,2048]{1,0:T(8,128)(2,1)S(1)}, bf16[1024,2048]{1,0:T(8,128)(2,1)}, u32[]{:S(2)}, u32[]{:S(2)}) collective-permute-start(bf16[1024,2048]{1,0:T(8,128)(2,1)S(1)} %subtract_convert_fusion), channel_id=1, source_target_pairs={{0,4},{4,8},{8,12},{12,16},{16,20},{20,24},{24,28},{28,32},{32,36}... | collective-permute-start | bytes 12582920 | tf_op jit(solution)/shard_map/ppermute | solution.py:12
  388.3 2.0 copy-start.3
Sparse Core Ops, SparseCore 0:
  23.5 40.8 reduce-scatter.1
  67.2 26.9 all-gather.1
where the time goes:
time: 425 us; the launch traced here: 424 us
  waiting for transfers between devices  328 us (77%)
  other arithmetic  32.8 us (8%)
  matrix products  31.3 us (7%)
  between operations  14.2 us (3%)
  starting transfers between devices  10.8 us (3%)
  local copies, waits for them, and re-layouts  6.84 us (2%)
    ppermute x4, waiting for transfers between devices, passed_along(): return lax.ppermute(value, axis, pairs)  263 us
    reduce_scatter x1, waiting for transfers between devices, local(): lax.psum_scatter(partial_value.astype(jnp.bfloat16), 'mp', scatter_dimens...  38.3 us
    all_gather x1, waiting for transfers between devices, local(): err_grad = lax.all_gather(err_own, 'mp', axis=0, tiled=True)  27.2 us
    ppermute x4, starting transfers between devices, passed_along(): return lax.ppermute(value, axis, pairs)  10.6 us
    broadcast_in_dim x1, other arithmetic, local(): return (w_gate[None], w_up[None], w_down[None])  10.1 us
    convert_element_type x1, other arithmetic, mix_three(): return (total / 3.0).astype(jnp.bfloat16)  9.17 us
  transfers between devices with their start and end apart: 6, of which 4 were waited for; matrix products, arithmetic and copies ran while one was open for 4% of the time, Pallas kernels for 0%

commit v1 on v0

v1 whole, which is shorter than its diff:
```python
import functools

import jax
import jax.numpy as jnp
from jax import lax
from jax.experimental import pallas as pl
from jax.experimental.pallas import tpu as pltpu
from jax.sharding import PartitionSpec as P

MESH = pl.DeviceIdType.MESH
F32 = jnp.float32
BF16 = jnp.bfloat16
COLS = 256
ROWS = 256


def dot(a, b, dims):
    return lax.dot_general(a, b, (dims, ((), ())), preferred_element_type=F32)


def kernel(
    replicas,
    tok_h, tgt_h, wg_h, wu_h, wd_h,
    og, ou, od, lo_h, hi_h,
    x, tg, nrm, wd, slope, act, hid, hid_t, err, gg, gu,
    part, part_in, sum_in, glo, ghi, ulo, uhi, stage,
    load_sem, w_sem, p_send, p_recv, q_send, q_recv, e_send, e_recv,
    d_send, d_recv, g_send, g_recv, u_send, u_recv, st_sem,
):
    g = lax.axis_index("gossip")
    m = lax.axis_index("mp")
    core = lax.rem(m, 2)
    sibling = m + 1 - 2 * core
    peer = lax.rem(m + 2, 4)
    after = lax.rem(g + 1, replicas)
    before = lax.rem(g + replicas - 1, replicas)
    toks, width = x.shape
    units = wd.shape[0]
    half = toks // 2
    in_scale = 1.0 / width**0.5
    mid_scale = 1.0 / (4 * units) ** 0.5
    step_size = (4 * units) / 4.0
    n_cols = width // COLS
    n_rows = width // ROWS
    n_units = units // COLS
    mine = pl.ds(pl.multiple_of(core * half, half), half)
    theirs = pl.ds(pl.multiple_of((1 - core) * half, half), half)

    def cols(i, size=COLS):
        return pl.ds(pl.multiple_of(i * size, size), size)

    tok_copy = pltpu.make_async_copy(tok_h, x, load_sem.at[0])
    tok_copy.start()

    def w_copies(f):
        return (
            pltpu.make_async_copy(wg_h.at[:, cols(f)], og.at[:, cols(f)], w_sem.at[0, f]),
            pltpu.make_async_copy(wu_h.at[:, cols(f)], ou.at[:, cols(f)], w_sem.at[1, f]),
        )

    for f in range(n_units):
        for copy in w_copies(f):
            copy.start()
    wd_copy = pltpu.make_async_copy(wd_h, wd, load_sem.at[1])
    wd_copy.start()
    tgt_copy = pltpu.make_async_copy(tgt_h.at[mine, :], tg, load_sem.at[2])
    tgt_copy.start()

    barrier = pltpu.get_barrier_semaphore()
    for where in ((g, sibling), (g, peer), (after, m), (before, m)):
        pl.semaphore_signal(barrier, inc=1, device_id=where, device_id_type=MESH)

    tok_copy.wait()

    def norm(i, carry):
        rows = pl.ds(pl.multiple_of(i * 64, 64), 64)
        wide = x[rows, :].astype(F32)
        mean = jnp.mean(wide * wide, axis=-1, keepdims=True)
        nrm[rows, :] = (wide * lax.rsqrt(mean + 1e-06)).astype(BF16)
        return carry

    lax.fori_loop(0, toks // 64, norm, 0)

    def forward(f, carry):
        for copy in w_copies(f):
            copy.wait()
        gate = dot(nrm[...], og[:, cols(f)], ((1,), (0,))) * in_scale
        up = dot(nrm[...], ou[:, cols(f)], ((1,), (0,))) * in_scale
        sig = jax.nn.sigmoid(gate)
        acted = gate * sig
        act[:, cols(f)] = acted
        slope[:, cols(f)] = up * (sig * (1.0 + gate * (1.0 - sig)))
        hid[:, cols(f)] = (acted * up).astype(BF16)
        return carry

    lax.fori_loop(0, n_units, forward, 0)
    wd_copy.wait()
    pl.semaphore_wait(barrier, 4)

    def p_copy(d):
        return pltpu.make_async_remote_copy(
            src_ref=part.at[theirs, cols(d)], dst_ref=part_in.at[:, cols(d)],
            send_sem=p_send.at[d], recv_sem=p_recv.at[d],
            device_id=(g, sibling), device_id_type=MESH,
        )

    def q_copy(d):
        return pltpu.make_async_remote_copy(
            src_ref=part.at[mine, cols(d)], dst_ref=sum_in.at[:, cols(d)],
            send_sem=q_send.at[d], recv_sem=q_recv.at[d],
            device_id=(g, peer), device_id_type=MESH,
        )

    def e_copy(d):
        return pltpu.make_async_remote_copy(
            src_ref=err.at[mine, cols(d)], dst_ref=err.at[mine, cols(d)],
            send_sem=e_send.at[d], recv_sem=e_recv.at[d],
            device_id=(g, sibling), device_id_type=MESH,
        )

    def pair(src, lo, hi, send, recv, i):
        return (
            pltpu.make_async_remote_copy(
                src_ref=src, dst_ref=lo, send_sem=send.at[0, i], recv_sem=recv.at[0, i],
                device_id=(after, m), device_id_type=MESH,
            ),
            pltpu.make_async_remote_copy(
                src_ref=src, dst_ref=hi, send_sem=send.at[1, i], recv_sem=recv.at[1, i],
                device_id=(before, m), device_id_type=MESH,
            ),
        )

    def d_copies(d):
        return pair(od.at[:, cols(d)], lo_h.at[d], hi_h.at[d], d_send, d_recv, d)

    def g_copies(i):
        rows = cols(i, ROWS)
        return pair(og.at[rows, :], glo.at[rows, :], ghi.at[rows, :], g_send, g_recv, i)

    def u_copies(i):
        rows = cols(i, ROWS)
        return pair(ou.at[rows, :], ulo.at[rows, :], uhi.at[rows, :], u_send, u_recv, i)

    def partial(d):
        part[:, cols(d)] = dot(hid[...], wd[:, cols(d)], ((1,), (0,))).astype(BF16)
        p_copy(d).start()

    def join(d):
        p_copy(d).wait()
        total = part[mine, cols(d)].astype(F32) + part_in[:, cols(d)].astype(F32)
        part[mine, cols(d)] = total.astype(BF16)
        q_copy(d).start()

    partial(0)
    partial(1)

    def spread(i, carry):
        join(i)
        partial(i + 2)
        return carry

    lax.fori_loop(0, n_cols - 2, spread, 0)
    join(n_cols - 2)
    join(n_cols - 1)

    def turn(i, carry):
        hid_t[cols(i), :] = hid[:, cols(i)].T
        return carry

    lax.fori_loop(0, n_units, turn, 0)
    tgt_copy.wait()

    def down(d, carry):
        q_copy(d).wait()
        total = part[mine, cols(d)].astype(F32) + sum_in[:, cols(d)].astype(F32)
        offset = x[mine, cols(d)].astype(F32) - tg[:, cols(d)].astype(F32)
        err[mine, cols(d)] = ((offset + total * mid_scale) / toks).astype(BF16)
        e_copy(d).start()
        e_copy(d).wait()
        grad = dot(hid_t[...], err[:, cols(d)], ((1,), (0,)))
        od[:, cols(d)] = (
            wd[:, cols(d)].astype(F32) - (step_size * mid_scale) * grad
        ).astype(BF16)
        for copy in d_copies(d):
            copy.start()
        return carry

    lax.fori_loop(0, n_cols, down, 0)

    def back(f, carry):
        grad = dot(err[...], wd[cols(f), :], ((1,), (1,))) * mid_scale
        gg[:, cols(f)] = (grad * slope[:, cols(f)]).astype(BF16)
        gu[:, cols(f)] = (grad * act[:, cols(f)]).astype(BF16)
        return carry

    lax.fori_loop(0, n_units, back, 0)

    def step(out, grads, copies):
        def one(i, carry):
            rows = cols(i, ROWS)
            grad = dot(nrm[:, rows], grads[...], ((0,), (0,)))
            out[rows, :] = (
                out[rows, :].astype(F32) - (step_size * in_scale) * grad
            ).astype(BF16)
            for copy in copies(i):
                copy.start()
            return carry

        lax.fori_loop(0, n_rows, one, 0)

    step(og, gg, g_copies)
    step(ou, gu, u_copies)

    def third(lo, own, hi):
        return ((lo.astype(F32) + own.astype(F32) + hi.astype(F32)) / 3.0).astype(BF16)

    def mix_down(d, carry):
        for copy in d_copies(d):
            copy.wait()
        loads = [
            pltpu.make_async_copy(lo_h.at[d], stage.at[0], st_sem.at[0]),
            pltpu.make_async_copy(hi_h.at[d], stage.at[1], st_sem.at[1]),
        ]
        for load in loads:
            load.start()
        for load in loads:
            load.wait()
        od[:, cols(d)] = third(stage[0], od[:, cols(d)], stage[1])
        return carry

    lax.fori_loop(0, n_cols, mix_down, 0)

    def mix(out, lo, hi, copies):
        def one(i, carry):
            rows = cols(i, ROWS)
            for copy in copies(i):
                copy.wait()
            out[rows, :] = third(lo[rows, :], out[rows, :], hi[rows, :])
            return carry

        lax.fori_loop(0, n_rows, one, 0)

    mix(og, glo, ghi, g_copies)
    mix(ou, ulo, uhi, u_copies)


def local(replicas, tokens, targets, gate_weight, up_weight, down_weight):
    toks, width = tokens.shape[1:]
    units = gate_weight.shape[2]
    n_cols, n_rows, n_units = width // COLS, width // ROWS, units // COLS
    half = toks // 2
    dma = pltpu.SemaphoreType.DMA
    any_spec = pl.BlockSpec(memory_space=pl.ANY)
    vmem_spec = pl.BlockSpec(memory_space=pltpu.VMEM)
    received = jax.ShapeDtypeStruct((n_cols, units, COLS), BF16)
    gate_out, up_out, down_out, _, _ = pl.pallas_call(
        functools.partial(kernel, replicas),
        out_shape=(
            pltpu.VMEM((width, units), BF16),
            pltpu.VMEM((width, units), BF16),
            pltpu.VMEM((units, width), BF16),
            received,
            received,
        ),
        in_specs=[any_spec] * 5,
        out_specs=(vmem_spec, vmem_spec, vmem_spec, any_spec, any_spec),
        scratch_shapes=[
            pltpu.VMEM((toks, width), BF16),
            pltpu.VMEM((half, width), BF16),
            pltpu.VMEM((toks, width), BF16),
            pltpu.VMEM((units, width), BF16),
            pltpu.VMEM((toks, units), F32),
            pltpu.VMEM((toks, units), F32),
            pltpu.VMEM((toks, units), BF16),
            pltpu.VMEM((units, toks), BF16),
            pltpu.VMEM((toks, width), BF16),
            pltpu.VMEM((toks, units), BF16),
            pltpu.VMEM((toks, units), BF16),
            pltpu.VMEM((toks, width), BF16),
            pltpu.VMEM((half, width), BF16),
            pltpu.VMEM((half, width), BF16),
            pltpu.VMEM((width, units), BF16),
            pltpu.VMEM((width, units), BF16),
            pltpu.VMEM((width, units), BF16),
            pltpu.VMEM((width, units), BF16),
            pltpu.VMEM((2, units, COLS), BF16),
            dma((3,)),
            dma((2, n_units)),
            dma((n_cols,)),
            dma((n_cols,)),
            dma((n_cols,)),
            dma((n_cols,)),
            dma((n_cols,)),
            dma((n_cols,)),
            dma((2, n_cols)),
            dma((2, n_cols)),
            dma((2, n_rows)),
            dma((2, n_rows)),
            dma((2, n_rows)),
            dma((2, n_rows)),
            dma((2,)),
        ],
        compiler_params=pltpu.CompilerParams(
            collective_id=0, has_side_effects=True, vmem_limit_bytes=50 * 2**20
        ),
    )(tokens[0], targets[0], gate_weight[0], up_weight[0], down_weight[0])
    return gate_out[None], up_out[None], down_out[None]


def solution(mesh):
    placed = (
        P("gossip", None, None),
        P("gossip", None, None),
        P("gossip", None, "mp"),
        P("gossip", None, "mp"),
        P("gossip", "mp", None),
    )
    return jax.shard_map(
        functools.partial(local, mesh.shape["gossip"]),
        mesh=mesh,
        in_specs=placed,
        out_specs=(P("gossip", None, "mp"), P("gossip", None, "mp"), P("gossip", "mp", None)),
        check_vma=False,
    )
```

time: 425 us -> 560 us (1.32)
  Pallas kernels: 0 us -> 553 us
  waiting for transfers between devices: 328 us -> 0 us
  other arithmetic: 32.8 us -> 0 us
  matrix products: 31.3 us -> 0 us
  between operations: 14.2 us -> 0.64 us
  starting transfers between devices: 10.8 us -> 0 us
    pallas_call x0 -> x1, Pallas kernels: none -> 553 us  [local(): pl.pallas_call(functools.partial(kernel, replicas), out_shape=(pltpu.VMEM...]
    ppermute x4 -> x0, waiting for transfers between devices: 263 us -> none  [passed_along(): return lax.ppermute(value, axis, pairs)]
    reduce_scatter x1 -> x0, waiting for transfers between devices: 38.3 us -> none  [local(): lax.psum_scatter(partial_value.astype(jnp.bfloat16), 'mp', scatter_dimens...]
    dot_general x7 -> x0, matrix products: 31.3 us -> none  [the longest x1 5.34 us: local(): jnp.dot(normed, w_gate, preferred_element_type=jnp.float32) * in_scale]
    all_gather x1 -> x0, waiting for transfers between devices: 27.2 us -> none  [local(): err_grad = lax.all_gather(err_own, 'mp', axis=0, tiled=True)]
    convert_element_type x3 -> x0, other arithmetic: 14.2 us -> none  [the longest x1 9.17 us: mix_three(): return (total / 3.0).astype(jnp.bfloat16)]
    ppermute x4 -> x0, starting transfers between devices: 10.6 us -> none  [passed_along(): return lax.ppermute(value, axis, pairs)]
    broadcast_in_dim x1 -> x0, other arithmetic: 10.1 us -> none  [local(): return (w_gate[None], w_up[None], w_down[None])]
  transfers between devices with their start and end apart: 6 -> 0, of which waited for: 4 -> 0; matrix products, arithmetic and copies ran while one was open for 4% -> 0% of each run, Pallas kernels for 0% -> 0%
where the time goes in v1:
time: 560 us
  Pallas kernels  553 us (99%)
  local copies, waits for them, and re-layouts  6.04 us (1%)
    pallas_call x1, Pallas kernels, local(): pl.pallas_call(functools.partial(kernel, replicas), out_shape=(pltpu.VMEM...  553 us

profile of v1, /device:TPU:1, one launch (start us, length us, event | category | flops | bytes accessed | tf_op | source)
XLA Modules:
  0.0 559.8 jit_solution(1192830888743512916)
XLA Ops:
  0.6 553.2 %shard_map.76 = (bf16[2048,1024]{1,0:T(8,128)(2,1)S(1)}, bf16[2048,1024]{1,0:T(8,128)(2,1)S(1)}, bf16[1024,2048]{1,0:T(8,128)(2,1)S(1)}, bf16[8,1024,256]{2,1,0:T(8,128)(2,1)}, bf16[8,1024,256]{2,1,0:T(8,128)(2,1)}) custom-call(bf16[512,2048]{1,0:T(8,128)(2,1)} %bitcast.14, bf16[512,2048]{1,0:T(8,128)(2,1)} %bitcast.15, bf16[2048,1024]{1,0:T(8,128)(2,1)} %bitcast.11, ...), custom_call_target="tpu_custom_call" | custom-call | tf_op jit(solution)/shard_map/pallas_call | solution.py:256
  553.8 2.0 copy.11
  555.8 2.0 copy.12
  557.8 2.0 copy.13

commit v2 on v1

--- a/solution.py
+++ b/solution.py
@@ -11,6 +11,7 @@
 F32 = jnp.float32
 BF16 = jnp.bfloat16
 COLS = 256
+X, Y = 4, 2
 ROWS = 256
 
 
@@ -25,7 +26,7 @@
     x, tg, nrm, wd, slope, act, hid, hid_t, err, gg, gu,
     part, part_in, sum_in, glo, ghi, ulo, uhi, stage,
     load_sem, w_sem, p_send, p_recv, q_send, q_recv, e_send, e_recv,
-    d_send, d_recv, g_send, g_recv, u_send, u_recv, st_sem,
+    d_send, d_recv, g_send, g_recv, u_send, u_recv, st_sem, go_sem,
 ):
     g = lax.axis_index("gossip")
     m = lax.axis_index("mp")
@@ -66,9 +67,35 @@
     tgt_copy = pltpu.make_async_copy(tgt_h.at[mine, :], tg, load_sem.at[2])
     tgt_copy.start()
 
+    along = lax.rem(g, X)
+    last_end = along == X - 1
+    first_end = along == 0
+    at_end = jnp.logical_or(last_end, first_end)
+    layer = g // (X * Y)
+    layers = replicas // (X * Y)
+    beyond = lax.rem(layer + (along // (X - 1)) * 2 - 1 + layers, layers)
+    facing = [
+        (at * (X * Y) + row * X + (X - 1 - along), shard)
+        for at in (layer, beyond)
+        for row in range(Y)
+        for shard in range(4)
+    ]
+
+    def tell(sem, wheres):
+        for where in wheres:
+            pl.semaphore_signal(sem, inc=1, device_id=where, device_id_type=MESH)
+
     barrier = pltpu.get_barrier_semaphore()
-    for where in ((g, sibling), (g, peer), (after, m), (before, m)):
-        pl.semaphore_signal(barrier, inc=1, device_id=where, device_id_type=MESH)
+    near = ((g, sibling), (g, peer))
+    inward = g + 1 - 2 * (along // (X - 1))
+
+    @pl.when(jnp.logical_not(at_end))
+    def _():
+        tell(barrier, (*near, (after, m), (before, m)))
+
+    @pl.when(at_end)
+    def _():
+        tell(barrier, (*near, (inward, m), *facing))
 
     tok_copy.wait()
 
@@ -95,7 +122,14 @@
 
     lax.fori_loop(0, n_units, forward, 0)
     wd_copy.wait()
-    pl.semaphore_wait(barrier, 4)
+
+    @pl.when(jnp.logical_not(at_end))
+    def _():
+        pl.semaphore_wait(barrier, len(near) + 2)
+
+    @pl.when(at_end)
+    def _():
+        pl.semaphore_wait(barrier, len(near) + 1 + len(facing))
 
     def p_copy(d):
         return pltpu.make_async_remote_copy(
@@ -172,6 +206,11 @@
 
     def down(d, carry):
         q_copy(d).wait()
+
+        @pl.when(jnp.logical_and(at_end, d == n_cols - 1))
+        def _():
+            tell(go_sem, facing)
+
         total = part[mine, cols(d)].astype(F32) + sum_in[:, cols(d)].astype(F32)
         offset = x[mine, cols(d)].astype(F32) - tg[:, cols(d)].astype(F32)
         err[mine, cols(d)] = ((offset + total * mid_scale) / toks).astype(BF16)
@@ -181,11 +220,24 @@
         od[:, cols(d)] = (
             wd[:, cols(d)].astype(F32) - (step_size * mid_scale) * grad
         ).astype(BF16)
-        for copy in d_copies(d):
-            copy.start()
+        ahead, behind = d_copies(d)
+        pl.when(jnp.logical_not(last_end))(ahead.start)
+        pl.when(jnp.logical_not(first_end))(behind.start)
         return carry
 
     lax.fori_loop(0, n_cols, down, 0)
+
+    @pl.when(at_end)
+    def _():
+        pl.semaphore_wait(go_sem, len(facing))
+
+    def held_back(d, carry):
+        ahead, behind = d_copies(d)
+        pl.when(last_end)(ahead.start)
+        pl.when(first_end)(behind.start)
+        return carry
+
+    lax.fori_loop(0, n_cols, held_back, 0)
 
     def back(f, carry):
         grad = dot(err[...], wd[cols(f), :], ((1,), (1,))) * mid_scale
@@ -299,6 +351,7 @@
             dma((2, n_rows)),
             dma((2, n_rows)),
             dma((2,)),
+            pltpu.SemaphoreType.REGULAR,
         ],
         compiler_params=pltpu.CompilerParams(
             collective_id=0, has_side_effects=True, vmem_limit_bytes=50 * 2**20

time: 560 us -> 327 us (0.58)
  Pallas kernels: 553 us -> 320 us
    pallas_call x1, Pallas kernels: 553 us -> 320 us  [local(): pl.pallas_call(functools.partial(kernel, replicas), out_shape=(pltpu.VMEM...]
where the time goes in v2:
time: 327 us
  Pallas kernels  320 us (98%)
  local copies, waits for them, and re-layouts  6.04 us (2%)
    pallas_call x1, Pallas kernels, local(): pl.pallas_call(functools.partial(kernel, replicas), out_shape=(pltpu.VMEM...  320 us

profile of v2, /device:TPU:1, one launch (start us, length us, event | category | flops | bytes accessed | tf_op | source)
XLA Modules:
  0.0 326.9 jit_solution(18152333007848936749)
XLA Ops:
  0.6 320.2 %shard_map.76 = (bf16[2048,1024]{1,0:T(8,128)(2,1)S(1)}, bf16[2048,1024]{1,0:T(8,128)(2,1)S(1)}, bf16[1024,2048]{1,0:T(8,128)(2,1)S(1)}, bf16[8,1024,256]{2,1,0:T(8,128)(2,1)}, bf16[8,1024,256]{2,1,0:T(8,128)(2,1)}) custom-call(bf16[512,2048]{1,0:T(8,128)(2,1)} %bitcast.14, bf16[512,2048]{1,0:T(8,128)(2,1)} %bitcast.15, bf16[2048,1024]{1,0:T(8,128)(2,1)} %bitcast.11, ...), custom_call_target="tpu_custom_call" | custom-call | tf_op jit(solution)/shard_map/pallas_call | solution.py:308
  320.8 2.0 copy.11
  322.8 2.0 copy.12
  324.8 2.0 copy.13

commit v3 on v2

--- a/solution.py
+++ b/solution.py
@@ -22,11 +22,11 @@
 def kernel(
     replicas,
     tok_h, tgt_h, wg_h, wu_h, wd_h,
-    og, ou, od, lo_h, hi_h,
+    og, ou, od, lo_h, hi_h, relay_h,
     x, tg, nrm, wd, slope, act, hid, hid_t, err, gg, gu,
     part, part_in, sum_in, glo, ghi, ulo, uhi, stage,
     load_sem, w_sem, p_send, p_recv, q_send, q_recv, e_send, e_recv,
-    d_send, d_recv, g_send, g_recv, u_send, u_recv, st_sem, go_sem,
+    d_send, d_recv, g_send, g_recv, u_send, u_recv, st_sem, relay_sem, go_sem,
 ):
     g = lax.axis_index("gossip")
     m = lax.axis_index("mp")
@@ -59,13 +59,10 @@
             pltpu.make_async_copy(wu_h.at[:, cols(f)], ou.at[:, cols(f)], w_sem.at[1, f]),
         )
 
-    for f in range(n_units):
-        for copy in w_copies(f):
-            copy.start()
+    for copy in w_copies(0):
+        copy.start()
     wd_copy = pltpu.make_async_copy(wd_h, wd, load_sem.at[1])
-    wd_copy.start()
     tgt_copy = pltpu.make_async_copy(tgt_h.at[mine, :], tg, load_sem.at[2])
-    tgt_copy.start()
 
     along = lax.rem(g, X)
     last_end = along == X - 1
@@ -86,7 +83,8 @@
             pl.semaphore_signal(sem, inc=1, device_id=where, device_id_type=MESH)
 
     barrier = pltpu.get_barrier_semaphore()
-    near = ((g, sibling), (g, peer))
+    two_away = lax.rem(g + (along // 2) * 4 - 2 + replicas, replicas)
+    near = ((g, sibling), (g, peer), (two_away, m))
     inward = g + 1 - 2 * (along // (X - 1))
 
     @pl.when(jnp.logical_not(at_end))
@@ -98,6 +96,11 @@
         tell(barrier, (*near, (inward, m), *facing))
 
     tok_copy.wait()
+    for f in range(1, n_units):
+        for copy in w_copies(f):
+            copy.start()
+    wd_copy.start()
+    tgt_copy.start()
 
     def norm(i, carry):
         rows = pl.ds(pl.multiple_of(i * 64, 64), 64)
@@ -174,6 +177,21 @@
     def u_copies(i):
         rows = cols(i, ROWS)
         return pair(ou.at[rows, :], ulo.at[rows, :], uhi.at[rows, :], u_send, u_recv, i)
+
+    def relay_out():
+        return pltpu.make_async_remote_copy(
+            src_ref=od.at[:, cols(0)], dst_ref=relay_h,
+            send_sem=relay_sem.at[0], recv_sem=relay_sem.at[1],
+            device_id=(two_away, m), device_id_type=MESH,
+        )
+
+    def relay_on(back):
+        dst, where = (lo_h, before) if back else (hi_h, after)
+        return pltpu.make_async_remote_copy(
+            src_ref=relay_h, dst_ref=dst.at[0],
+            send_sem=relay_sem.at[2], recv_sem=d_recv.at[0 if back else 1, 0],
+            device_id=(where, m), device_id_type=MESH,
+        )
 
     def partial(d):
         part[:, cols(d)] = dot(hid[...], wd[:, cols(d)], ((1,), (0,))).astype(BF16)
@@ -223,6 +241,7 @@
         ahead, behind = d_copies(d)
         pl.when(jnp.logical_not(last_end))(ahead.start)
         pl.when(jnp.logical_not(first_end))(behind.start)
+        pl.when(jnp.logical_and(at_end, d == 0))(relay_out().start)
         return carry
 
     lax.fori_loop(0, n_cols, down, 0)
@@ -237,7 +256,7 @@
         pl.when(first_end)(behind.start)
         return carry
 
-    lax.fori_loop(0, n_cols, held_back, 0)
+    lax.fori_loop(1, n_cols, held_back, 0)
 
     def back(f, carry):
         grad = dot(err[...], wd[cols(f), :], ((1,), (1,))) * mid_scale
@@ -261,14 +280,27 @@
         lax.fori_loop(0, n_rows, one, 0)
 
     step(og, gg, g_copies)
+
+    @pl.when(jnp.logical_not(at_end))
+    def _():
+        relay_out().wait_recv()
+        pl.when(along == 1)(relay_on(True).start)
+        pl.when(along == 2)(relay_on(False).start)
+
     step(ou, gu, u_copies)
 
     def third(lo, own, hi):
         return ((lo.astype(F32) + own.astype(F32) + hi.astype(F32)) / 3.0).astype(BF16)
 
-    def mix_down(d, carry):
-        for copy in d_copies(d):
-            copy.wait()
+    def mix_down(i, carry):
+        d = lax.rem(i + 1, n_cols)
+        ahead, behind = d_copies(d)
+        ahead.wait_recv()
+        behind.wait_recv()
+        relayed = jnp.logical_and(at_end, d == 0)
+        pl.when(relayed)(relay_out().wait_send)
+        pl.when(jnp.logical_not(jnp.logical_and(last_end, d == 0)))(ahead.wait_send)
+        pl.when(jnp.logical_not(jnp.logical_and(first_end, d == 0)))(behind.wait_send)
         loads = [
             pltpu.make_async_copy(lo_h.at[d], stage.at[0], st_sem.at[0]),
             pltpu.make_async_copy(hi_h.at[d], stage.at[1], st_sem.at[1]),
@@ -292,8 +324,38 @@
 
         lax.fori_loop(0, n_rows, one, 0)
 
+    pl.when(along == 1)(relay_on(True).wait_send)
+    pl.when(along == 2)(relay_on(False).wait_send)
     mix(og, glo, ghi, g_copies)
     mix(ou, ulo, uhi, u_copies)
+
+
+def write_kernel(pieces, *refs):
+    held, out, sem = refs[:3], refs[3:6], refs[6]
+    copies = []
+    for i in range(3):
+        rows = held[i].shape[0] // pieces
+        for p in range(pieces):
+            part = pl.ds(p * rows, rows)
+            copies.append(
+                pltpu.make_async_copy(held[i].at[part, :], out[i].at[0, part, :], sem.at[i, p])
+            )
+    for copy in copies:
+        copy.start()
+    for copy in copies:
+        copy.wait()
+
+
+def write_out(*arrays):
+    pieces = 4
+    return pl.pallas_call(
+        functools.partial(write_kernel, pieces),
+        out_shape=tuple(jax.ShapeDtypeStruct((1, *a.shape), a.dtype) for a in arrays),
+        in_specs=[pl.BlockSpec(memory_space=pltpu.VMEM)] * 3,
+        out_specs=(pl.BlockSpec(memory_space=pl.ANY),) * 3,
+        scratch_shapes=[pltpu.SemaphoreType.DMA((3, pieces))],
+        compiler_params=pltpu.CompilerParams(vmem_limit_bytes=16 * 2**20),
+    )(*arrays)
 
 
 def local(replicas, tokens, targets, gate_weight, up_weight, down_weight):
@@ -305,7 +367,7 @@
     any_spec = pl.BlockSpec(memory_space=pl.ANY)
     vmem_spec = pl.BlockSpec(memory_space=pltpu.VMEM)
     received = jax.ShapeDtypeStruct((n_cols, units, COLS), BF16)
-    gate_out, up_out, down_out, _, _ = pl.pallas_call(
+    gate_out, up_out, down_out, *_ = pl.pallas_call(
         functools.partial(kernel, replicas),
         out_shape=(
             pltpu.VMEM((width, units), BF16),
@@ -313,9 +375,10 @@
             pltpu.VMEM((units, width), BF16),
             received,
             received,
+            jax.ShapeDtypeStruct((units, COLS), BF16),
         ),
         in_specs=[any_spec] * 5,
-        out_specs=(vmem_spec, vmem_spec, vmem_spec, any_spec, any_spec),
+        out_specs=(vmem_spec, vmem_spec, vmem_spec, any_spec, any_spec, any_spec),
         scratch_shapes=[
             pltpu.VMEM((toks, width), BF16),
             pltpu.VMEM((half, width), BF16),
@@ -351,13 +414,14 @@
             dma((2, n_rows)),
             dma((2, n_rows)),
             dma((2,)),
+            dma((3,)),
             pltpu.SemaphoreType.REGULAR,
         ],
         compiler_params=pltpu.CompilerParams(
             collective_id=0, has_side_effects=True, vmem_limit_bytes=50 * 2**20
         ),
     )(tokens[0], targets[0], gate_weight[0], up_weight[0], down_weight[0])
-    return gate_out[None], up_out[None], down_out[None]
+    return write_out(gate_out, up_out, down_out)
 
 
 def solution(mesh):

time: 327 us -> 313 us (0.957)
  Pallas kernels: 320 us -> 312 us
  local copies, waits for them, and re-layouts: 6.04 us -> 0 us
    pallas_call x1, Pallas kernels: 320 us -> 308 us  [local(): pl.pallas_call(functools.partial(kernel, replicas), out_shape=(pltpu.VMEM...]
    unnamed x3 -> x0, local copies, waits for them, and re-layouts: 6.04 us -> none
    pallas_call x0 -> x1, Pallas kernels: none -> 4.67 us  [write_out(): pl.pallas_call(functools.partial(write_kernel, pieces), out_shape=tuple((...]
where the time goes in v3:
time: 313 us
  Pallas kernels  312 us (100%)
    pallas_call x1, Pallas kernels, local(): pl.pallas_call(functools.partial(kernel, replicas), out_shape=(pltpu.VMEM...  308 us

profile of v3, /device:TPU:1, one launch (start us, length us, event | category | flops | bytes accessed | tf_op | source)
XLA Modules:
  0.0 313.0 jit_solution(13456744710208723688)
XLA Ops:
  0.6 307.7 %shard_map.76 = (bf16[2048,1024]{1,0:T(8,128)(2,1)S(1)}, bf16[2048,1024]{1,0:T(8,128)(2,1)S(1)}, bf16[1024,2048]{1,0:T(8,128)(2,1)S(1)}, bf16[8,1024,256]{2,1,0:...) custom-call(bf16[512,2048]{1,0:T(8,128)(2,1)} %bitcast.8, bf16[512,2048]{1,0:T(8,128)(2,1)} %bitcast.9, ...), custom_call_target="tpu_custom_call" | custom-call | tf_op jit(solution)/shard_map/pallas_call | solution.py:370
  308.3 4.7 %shard_map.77 = (bf16[1,2048,1024]{2,1,0:T(8,128)(2,1)}, bf16[1,2048,1024]{2,1,0:T(8,128)(2,1)}, bf16[1,1024,2048]{2,1,0:T(8,128)(2,1)}) custom-call(bf16[2048,1024]{1,0:T(8,128)(2,1)S(1)} %get-tuple-element.6.refs_0_, bf16[2048,1024]{1,0:T(8,128)(2,1)S(1)} %get-tuple-element.7.refs_1_, bf16[1024,2048]{1,0:T(8,128)(2,1)S(1)} %get-tuple-element.8.refs_2_), custom_call_target="tpu_custom_call" | custom-call | tf_op jit(solution)/shard_map/pallas_call | solution.py:351

commit v4 on v3

--- a/solution.py
+++ b/solution.py
@@ -13,6 +13,9 @@
 COLS = 256
 X, Y = 4, 2
 ROWS = 256
+REST = 304
+AWAY = 224
+FIRST = 128
 
 
 def dot(a, b, dims):
@@ -23,10 +26,11 @@
     replicas,
     tok_h, tgt_h, wg_h, wu_h, wd_h,
     og, ou, od, lo_h, hi_h, relay_h,
-    x, tg, nrm, wd, slope, act, hid, hid_t, err, gg, gu,
-    part, part_in, sum_in, glo, ghi, ulo, uhi, stage,
-    load_sem, w_sem, p_send, p_recv, q_send, q_recv, e_send, e_recv,
-    d_send, d_recv, g_send, g_recv, u_send, u_recv, st_sem, relay_sem, go_sem,
+    x, tg, inv, nrm, wd, slope, act, hid, hid_t, err, gg, gu,
+    part, part_in, sum_in, glo, ghi, ulo, uhi, stage, crossing, summing,
+    tok_sem, load_sem, w_sem, p_send, p_recv, q_send, q_recv, e_send, e_recv,
+    d_send, d_recv, g_send, g_recv, u_send, u_recv, st_sem,
+    b_send, b_recv, relay_sem, cross_sem, go_sem,
 ):
     g = lax.axis_index("gossip")
     m = lax.axis_index("mp")
@@ -41,17 +45,27 @@
     in_scale = 1.0 / width**0.5
     mid_scale = 1.0 / (4 * units) ** 0.5
     step_size = (4 * units) / 4.0
+
+    def cols(i, size=COLS):
+        return pl.ds(pl.multiple_of(i * size, size), size)
+
     n_cols = width // COLS
     n_rows = width // ROWS
+    n_rest = (width - AWAY) // REST
+    rows_b = pl.ds(0, AWAY)
+    early, late = pl.ds(0, FIRST), pl.ds(FIRST, COLS - FIRST)
     n_units = units // COLS
     mine = pl.ds(pl.multiple_of(core * half, half), half)
     theirs = pl.ds(pl.multiple_of((1 - core) * half, half), half)
 
-    def cols(i, size=COLS):
-        return pl.ds(pl.multiple_of(i * size, size), size)
-
-    tok_copy = pltpu.make_async_copy(tok_h, x, load_sem.at[0])
-    tok_copy.start()
+    piece = toks // 4
+
+    def tok_copy(i):
+        rows = cols(i, piece)
+        return pltpu.make_async_copy(tok_h.at[rows, :], x.at[rows, :], tok_sem.at[i])
+
+    for i in range(4):
+        tok_copy(i).start()
 
     def w_copies(f):
         return (
@@ -61,8 +75,9 @@
 
     for copy in w_copies(0):
         copy.start()
-    wd_copy = pltpu.make_async_copy(wd_h, wd, load_sem.at[1])
-    tgt_copy = pltpu.make_async_copy(tgt_h.at[mine, :], tg, load_sem.at[2])
+
+    wd_copy = pltpu.make_async_copy(wd_h, wd, load_sem.at[0])
+    tgt_copy = pltpu.make_async_copy(tgt_h.at[mine, :], tg, load_sem.at[1])
 
     along = lax.rem(g, X)
     last_end = along == X - 1
@@ -83,39 +98,40 @@
             pl.semaphore_signal(sem, inc=1, device_id=where, device_id_type=MESH)
 
     barrier = pltpu.get_barrier_semaphore()
-    two_away = lax.rem(g + (along // 2) * 4 - 2 + replicas, replicas)
-    near = ((g, sibling), (g, peer), (two_away, m))
+    far_end = g + (X - 1) * (1 - 2 * (along // (X - 1)))
+    diagonal = lax.rem(g + (X + 1) * (1 - 2 * lax.rem(along, 2)) + replicas, replicas)
+    across_up = lax.rem(g + X, replicas)
+    across_down = lax.rem(g - X + replicas, replicas)
+    near = ((g, sibling), (g, peer), (diagonal, m))
     inward = g + 1 - 2 * (along // (X - 1))
 
     @pl.when(jnp.logical_not(at_end))
     def _():
-        tell(barrier, (*near, (after, m), (before, m)))
+        tell(barrier, (*near, (after, m), (before, m), (across_up, m), (across_down, m)))
 
     @pl.when(at_end)
     def _():
         tell(barrier, (*near, (inward, m), *facing))
 
-    tok_copy.wait()
-    for f in range(1, n_units):
-        for copy in w_copies(f):
-            copy.start()
-    wd_copy.start()
-    tgt_copy.start()
-
-    def norm(i, carry):
-        rows = pl.ds(pl.multiple_of(i * 64, 64), 64)
+    def square(i, carry):
+        rows = cols(i, 64)
         wide = x[rows, :].astype(F32)
         mean = jnp.mean(wide * wide, axis=-1, keepdims=True)
-        nrm[rows, :] = (wide * lax.rsqrt(mean + 1e-06)).astype(BF16)
-        return carry
-
-    lax.fori_loop(0, toks // 64, norm, 0)
+        inv[rows, :] = lax.rsqrt(mean + 1e-06)
+        return carry
+
+    for i in range(4):
+        tok_copy(i).wait()
+        lax.fori_loop(i * piece // 64, (i + 1) * piece // 64, square, 0)
+        for copy in w_copies(i + 1) if i + 1 < n_units else (wd_copy, tgt_copy):
+            copy.start()
 
     def forward(f, carry):
         for copy in w_copies(f):
             copy.wait()
-        gate = dot(nrm[...], og[:, cols(f)], ((1,), (0,))) * in_scale
-        up = dot(nrm[...], ou[:, cols(f)], ((1,), (0,))) * in_scale
+        scale = inv[...] * in_scale
+        gate = dot(x[...], og[:, cols(f)], ((1,), (0,))) * scale
+        up = dot(x[...], ou[:, cols(f)], ((1,), (0,))) * scale
         sig = jax.nn.sigmoid(gate)
         acted = gate * sig
         act[:, cols(f)] = acted
@@ -128,7 +144,7 @@
 
     @pl.when(jnp.logical_not(at_end))
     def _():
-        pl.semaphore_wait(barrier, len(near) + 2)
+        pl.semaphore_wait(barrier, len(near) + 4)
 
     @pl.when(at_end)
     def _():
@@ -156,13 +172,16 @@
         )
 
     def pair(src, lo, hi, send, recv, i):
+        def sem(sems, k):
+            return sems.at[k] if i is None else sems.at[k, i]
+
         return (
             pltpu.make_async_remote_copy(
-                src_ref=src, dst_ref=lo, send_sem=send.at[0, i], recv_sem=recv.at[0, i],
+                src_ref=src, dst_ref=lo, send_sem=sem(send, 0), recv_sem=sem(recv, 0),
                 device_id=(after, m), device_id_type=MESH,
             ),
             pltpu.make_async_remote_copy(
-                src_ref=src, dst_ref=hi, send_sem=send.at[1, i], recv_sem=recv.at[1, i],
+                src_ref=src, dst_ref=hi, send_sem=sem(send, 1), recv_sem=sem(recv, 1),
                 device_id=(before, m), device_id_type=MESH,
             ),
         )
@@ -170,28 +189,54 @@
     def d_copies(d):
         return pair(od.at[:, cols(d)], lo_h.at[d], hi_h.at[d], d_send, d_recv, d)
 
+    def g_pair(rows, send, recv, i):
+        return pair(og.at[rows, :], glo.at[rows, :], ghi.at[rows, :], send, recv, i)
+
+    def rest(i):
+        return pl.ds(pl.multiple_of(AWAY + i * REST, 16), REST)
+
     def g_copies(i):
-        rows = cols(i, ROWS)
-        return pair(og.at[rows, :], glo.at[rows, :], ghi.at[rows, :], g_send, g_recv, i)
+        return g_pair(rest(i), g_send, g_recv, i)
+
+    def b_copies():
+        return g_pair(rows_b, b_send, b_recv, None)
 
     def u_copies(i):
         rows = cols(i, ROWS)
         return pair(ou.at[rows, :], ulo.at[rows, :], uhi.at[rows, :], u_send, u_recv, i)
 
+    def send(src, dst, send_sem, recv_sem, replica):
+        return pltpu.make_async_remote_copy(
+            src_ref=src, dst_ref=dst, send_sem=send_sem, recv_sem=recv_sem,
+            device_id=(replica, m), device_id_type=MESH,
+        )
+
     def relay_out():
-        return pltpu.make_async_remote_copy(
-            src_ref=od.at[:, cols(0)], dst_ref=relay_h,
-            send_sem=relay_sem.at[0], recv_sem=relay_sem.at[1],
-            device_id=(two_away, m), device_id_type=MESH,
-        )
-
-    def relay_on(back):
-        dst, where = (lo_h, before) if back else (hi_h, after)
-        return pltpu.make_async_remote_copy(
-            src_ref=relay_h, dst_ref=dst.at[0],
-            send_sem=relay_sem.at[2], recv_sem=d_recv.at[0 if back else 1, 0],
-            device_id=(where, m), device_id_type=MESH,
-        )
+        return send(od.at[:, early], relay_h, relay_sem.at[0], relay_sem.at[1], far_end)
+
+    def relay_over():
+        return send(relay_h, relay_h, relay_sem.at[2], relay_sem.at[1], diagonal)
+
+    def relay_on(first):
+        dst, k, where = (lo_h, 0, before) if first else (hi_h, 1, after)
+        return send(relay_h, dst.at[0, :, early], relay_sem.at[2], d_recv.at[k, 0], where)
+
+    def late_copies():
+        return (
+            send(od.at[:, late], lo_h.at[0, :, late], d_send.at[0, 0], d_recv.at[0, 0], after),
+            send(od.at[:, late], hi_h.at[0, :, late], d_send.at[1, 0], d_recv.at[1, 0], before),
+        )
+
+    def cross_out(first):
+        src, where = (glo, across_down) if first else (ghi, across_up)
+        return send(src.at[rows_b, :], crossing, cross_sem.at[0], cross_sem.at[1], where)
+
+    def cross_in(first):
+        return send(crossing, summing, cross_sem.at[2], cross_sem.at[3], after if first else before)
+
+    def cross_end(first):
+        dst, where = (ghi, before) if first else (glo, after)
+        return send(summing, dst.at[rows_b, :], cross_sem.at[4], cross_sem.at[5], where)
 
     def partial(d):
         part[:, cols(d)] = dot(hid[...], wd[:, cols(d)], ((1,), (0,))).astype(BF16)
@@ -220,6 +265,13 @@
         return carry
 
     lax.fori_loop(0, n_units, turn, 0)
+
+    def norm(i, carry):
+        rows = cols(i, 64)
+        nrm[rows, :] = (x[rows, :].astype(F32) * inv[rows, :]).astype(BF16)
+        return carry
+
+    lax.fori_loop(0, toks // 64, norm, 0)
     tgt_copy.wait()
 
     def down(d, carry):
@@ -256,6 +308,9 @@
         pl.when(first_end)(behind.start)
         return carry
 
+    ahead, behind = late_copies()
+    pl.when(last_end)(ahead.start)
+    pl.when(first_end)(behind.start)
     lax.fori_loop(1, n_cols, held_back, 0)
 
     def back(f, carry):
@@ -266,41 +321,57 @@
 
     lax.fori_loop(0, n_units, back, 0)
 
-    def step(out, grads, copies):
-        def one(i, carry):
-            rows = cols(i, ROWS)
-            grad = dot(nrm[:, rows], grads[...], ((0,), (0,)))
-            out[rows, :] = (
-                out[rows, :].astype(F32) - (step_size * in_scale) * grad
-            ).astype(BF16)
-            for copy in copies(i):
-                copy.start()
-            return carry
-
-        lax.fori_loop(0, n_rows, one, 0)
-
-    step(og, gg, g_copies)
-
-    @pl.when(jnp.logical_not(at_end))
+    @pl.when(at_end)
     def _():
         relay_out().wait_recv()
-        pl.when(along == 1)(relay_on(True).start)
-        pl.when(along == 2)(relay_on(False).start)
-
-    step(ou, gu, u_copies)
+        relay_over().start()
+
+    def step(out, grads, rows):
+        grad = dot(nrm[:, rows], grads[...], ((0,), (0,)))
+        out[rows, :] = (out[rows, :].astype(F32) - (step_size * in_scale) * grad).astype(BF16)
+
+    def step_up(i, carry):
+        step(ou, gu, cols(i, ROWS))
+        return carry
+
+    def send_up(i, carry):
+        for copy in u_copies(i):
+            copy.start()
+        return carry
+
+    lower, upper = along <= 1, along >= 2
+    inside = jnp.logical_not(at_end)
+    first_in, last_in = along == 1, along == 2
+
+    def step_gate(i, carry):
+        step(og, gg, pl.ds(pl.multiple_of(i * 128, 128), 128))
+        return carry
+
+    def send_gate(i, carry):
+        for copy in g_copies(i):
+            copy.start()
+        return carry
+
+    lax.fori_loop(0, width // 128, step_gate, 0)
+    ahead, behind = b_copies()
+    pl.when(lower)(ahead.start)
+    pl.when(upper)(behind.start)
+    lax.fori_loop(0, n_rest, send_gate, 0)
+    lax.fori_loop(0, n_rows, step_up, 0)
 
     def third(lo, own, hi):
         return ((lo.astype(F32) + own.astype(F32) + hi.astype(F32)) / 3.0).astype(BF16)
 
-    def mix_down(i, carry):
-        d = lax.rem(i + 1, n_cols)
+    def mix_down(d, carry):
         ahead, behind = d_copies(d)
         ahead.wait_recv()
         behind.wait_recv()
-        relayed = jnp.logical_and(at_end, d == 0)
-        pl.when(relayed)(relay_out().wait_send)
         pl.when(jnp.logical_not(jnp.logical_and(last_end, d == 0)))(ahead.wait_send)
         pl.when(jnp.logical_not(jnp.logical_and(first_end, d == 0)))(behind.wait_send)
+        ahead, behind = late_copies()
+        pl.when(jnp.logical_and(last_end, d == 0))(ahead.wait_send)
+        pl.when(jnp.logical_and(first_end, d == 0))(behind.wait_send)
+        pl.when(jnp.logical_and(at_end, d == 0))(relay_out().wait_send)
         loads = [
             pltpu.make_async_copy(lo_h.at[d], stage.at[0], st_sem.at[0]),
             pltpu.make_async_copy(hi_h.at[d], stage.at[1], st_sem.at[1]),
@@ -312,22 +383,75 @@
         od[:, cols(d)] = third(stage[0], od[:, cols(d)], stage[1])
         return carry
 
-    lax.fori_loop(0, n_cols, mix_down, 0)
-
-    def mix(out, lo, hi, copies):
-        def one(i, carry):
-            rows = cols(i, ROWS)
-            for copy in copies(i):
-                copy.wait()
-            out[rows, :] = third(lo[rows, :], out[rows, :], hi[rows, :])
-            return carry
-
-        lax.fori_loop(0, n_rows, one, 0)
-
-    pl.when(along == 1)(relay_on(True).wait_send)
-    pl.when(along == 2)(relay_on(False).wait_send)
-    mix(og, glo, ghi, g_copies)
-    mix(ou, ulo, uhi, u_copies)
+    lax.fori_loop(1, n_cols, mix_down, 0)
+
+    @pl.when(inside)
+    def _():
+        relay_out().wait_recv()
+        pl.when(first_in)(relay_on(True).start)
+        pl.when(last_in)(relay_on(False).start)
+        for copy in b_copies():
+            copy.wait_recv()
+        pl.when(first_in)(cross_out(True).start)
+        pl.when(last_in)(cross_out(False).start)
+        cross_out(True).wait_recv()
+        pl.when(first_in)(cross_in(True).start)
+        pl.when(last_in)(cross_in(False).start)
+
+    lax.fori_loop(0, n_rows, send_up, 0)
+
+    def mix(out, lo, hi, rows):
+        out[rows, :] = third(lo[rows, :], out[rows, :], hi[rows, :])
+
+    def mix_gate(i, carry):
+        for copy in g_copies(i):
+            copy.wait()
+        mix(og, glo, ghi, rest(i))
+        return carry
+
+    lax.fori_loop(0, n_rest, mix_gate, 0)
+    lax.fori_loop(0, 1, mix_down, 0)
+    ahead, behind = b_copies()
+    pl.when(lower)(ahead.wait_send)
+    pl.when(upper)(behind.wait_send)
+
+    @pl.when(inside)
+    def _():
+        cross_in(True).wait_recv()
+        both = summing[...].astype(F32) + og[rows_b, :].astype(F32)
+        summing[...] = both.astype(BF16)
+        pl.when(first_in)(cross_end(True).start)
+        pl.when(last_in)(cross_end(False).start)
+        cross_out(True).wait_send()
+        mix(og, glo, ghi, rows_b)
+
+    def mix_up(i, carry):
+        for copy in u_copies(i):
+            copy.wait()
+        mix(ou, ulo, uhi, cols(i, ROWS))
+        return carry
+
+    lax.fori_loop(0, n_rows, mix_up, 0)
+
+    def end(own, both):
+        return ((own.astype(F32) + both.astype(F32)) / 3.0).astype(BF16)
+
+    relay_over().wait_send()
+
+    @pl.when(inside)
+    def _():
+        cross_in(True).wait_send()
+        cross_end(True).wait_send()
+
+    @pl.when(first_end)
+    def _():
+        cross_end(True).wait_recv()
+        og[rows_b, :] = end(og[rows_b, :], ghi[rows_b, :])
+
+    @pl.when(last_end)
+    def _():
+        cross_end(False).wait_recv()
+        og[rows_b, :] = end(og[rows_b, :], glo[rows_b, :])
 
 
 def write_kernel(pieces, *refs):
@@ -362,6 +486,7 @@
     toks, width = tokens.shape[1:]
     units = gate_weight.shape[2]
     n_cols, n_rows, n_units = width // COLS, width // ROWS, units // COLS
+    n_rest = (width - AWAY) // REST
     half = toks // 2
     dma = pltpu.SemaphoreType.DMA
     any_spec = pl.BlockSpec(memory_space=pl.ANY)
@@ -375,13 +500,14 @@
             pltpu.VMEM((units, width), BF16),
             received,
             received,
-            jax.ShapeDtypeStruct((units, COLS), BF16),
+            jax.ShapeDtypeStruct((units, FIRST), BF16),
         ),
         in_specs=[any_spec] * 5,
         out_specs=(vmem_spec, vmem_spec, vmem_spec, any_spec, any_spec, any_spec),
         scratch_shapes=[
             pltpu.VMEM((toks, width), BF16),
             pltpu.VMEM((half, width), BF16),
+            pltpu.VMEM((toks, 1), F32),
             pltpu.VMEM((toks, width), BF16),
             pltpu.VMEM((units, width), BF16),
             pltpu.VMEM((toks, units), F32),
@@ -399,7 +525,10 @@
             pltpu.VMEM((width, units), BF16),
             pltpu.VMEM((width, units), BF16),
             pltpu.VMEM((2, units, COLS), BF16),
-            dma((3,)),
+            pltpu.VMEM((AWAY, units), BF16),
+            pltpu.VMEM((AWAY, units), BF16),
+            dma((4,)),
+            dma((2,)),
             dma((2, n_units)),
             dma((n_cols,)),
             dma((n_cols,)),
@@ -409,12 +538,15 @@
             dma((n_cols,)),
             dma((2, n_cols)),
             dma((2, n_cols)),
-            dma((2, n_rows)),
-            dma((2, n_rows)),
+            dma((2, n_rest)),
+            dma((2, n_rest)),
             dma((2, n_rows)),
             dma((2, n_rows)),
             dma((2,)),
+            dma((2,)),
+            dma((2,)),
             dma((3,)),
+            dma((6,)),
             pltpu.SemaphoreType.REGULAR,
         ],
         compiler_params=pltpu.CompilerParams(

time: 313 us -> 308 us (0.984)
  Pallas kernels: 312 us -> 307 us
    pallas_call x1, Pallas kernels: 308 us -> 303 us  [local(): pl.pallas_call(functools.partial(kernel, replicas), out_shape=(pltpu.VMEM...]
where the time goes in v4:
time: 308 us
  Pallas kernels  307 us (100%)
    pallas_call x1, Pallas kernels, local(): pl.pallas_call(functools.partial(kernel, replicas), out_shape=(pltpu.VMEM...  303 us

profile of v4, /device:TPU:1, one launch (start us, length us, event | category | flops | bytes accessed | tf_op | source)
XLA Modules:
  0.0 307.9 jit_solution(9944801332902779656)
XLA Ops:
  0.6 302.6 %shard_map.76 = (bf16[2048,1024]{1,0:T(8,128)(2,1)S(1)}, bf16[2048,1024]{1,0:T(8,128)(2,1)S(1)}, bf16[1024,2048]{1,0:T(8,128)(2,1)S(1)}, bf16[8,1024,256]{2,1,0:...) custom-call(bf16[512,2048]{1,0:T(8,128)(2,1)} %bitcast.8, bf16[512,2048]{1,0:T(8,128)(2,1)} %bitcast.9, ...), custom_call_target="tpu_custom_call" | custom-call | tf_op jit(solution)/shard_map/pallas_call | solution.py:495
  303.2 4.7 %shard_map.77 = (bf16[1,2048,1024]{2,1,0:T(8,128)(2,1)}, bf16[1,2048,1024]{2,1,0:T(8,128)(2,1)}, bf16[1,1024,2048]{2,1,0:T(8,128)(2,1)}) custom-call(bf16[2048,1024]{1,0:T(8,128)(2,1)S(1)} %get-tuple-element.6.refs_0_, bf16[2048,1024]{1,0:T(8,128)(2,1)S(1)} %get-tuple-element.7.refs_1_, bf16[1024,2048]{1,0:T(8,128)(2,1)S(1)} %get-tuple-element.8.refs_2_), custom_call_target="tpu_custom_call" | custom-call | tf_op jit(solution)/shard_map/pallas_call | solution.py:475

commit v5 on v4

--- a/solution.py
+++ b/solution.py
@@ -13,9 +13,10 @@
 COLS = 256
 X, Y = 4, 2
 ROWS = 256
-REST = 304
-AWAY = 224
-FIRST = 128
+REST = 368
+AWAY = 208
+FIRST = 768
+HEAD = 128
 
 
 def dot(a, b, dims):
@@ -53,7 +54,7 @@
     n_rows = width // ROWS
     n_rest = (width - AWAY) // REST
     rows_b = pl.ds(0, AWAY)
-    early, late = pl.ds(0, FIRST), pl.ds(FIRST, COLS - FIRST)
+    early, late = pl.ds(0, FIRST), pl.ds(FIRST, units - FIRST)
     n_units = units // COLS
     mine = pl.ds(pl.multiple_of(core * half, half), half)
     theirs = pl.ds(pl.multiple_of((1 - core) * half, half), half)
@@ -150,24 +151,24 @@
     def _():
         pl.semaphore_wait(barrier, len(near) + 1 + len(facing))
 
-    def p_copy(d):
+    def p_copy(at, k):
         return pltpu.make_async_remote_copy(
-            src_ref=part.at[theirs, cols(d)], dst_ref=part_in.at[:, cols(d)],
-            send_sem=p_send.at[d], recv_sem=p_recv.at[d],
+            src_ref=part.at[theirs, at], dst_ref=part_in.at[:, at],
+            send_sem=p_send.at[k], recv_sem=p_recv.at[k],
             device_id=(g, sibling), device_id_type=MESH,
         )
 
-    def q_copy(d):
+    def q_copy(at, k):
         return pltpu.make_async_remote_copy(
-            src_ref=part.at[mine, cols(d)], dst_ref=sum_in.at[:, cols(d)],
-            send_sem=q_send.at[d], recv_sem=q_recv.at[d],
+            src_ref=part.at[mine, at], dst_ref=sum_in.at[:, at],
+            send_sem=q_send.at[k], recv_sem=q_recv.at[k],
             device_id=(g, peer), device_id_type=MESH,
         )
 
-    def e_copy(d):
+    def e_copy(at, k):
         return pltpu.make_async_remote_copy(
-            src_ref=err.at[mine, cols(d)], dst_ref=err.at[mine, cols(d)],
-            send_sem=e_send.at[d], recv_sem=e_recv.at[d],
+            src_ref=err.at[mine, at], dst_ref=err.at[mine, at],
+            send_sem=e_send.at[k], recv_sem=e_recv.at[k],
             device_id=(g, sibling), device_id_type=MESH,
         )
 
@@ -212,19 +213,19 @@
         )
 
     def relay_out():
-        return send(od.at[:, early], relay_h, relay_sem.at[0], relay_sem.at[1], far_end)
+        return send(od.at[early, cols(0)], relay_h, relay_sem.at[0], relay_sem.at[1], far_end)
 
     def relay_over():
         return send(relay_h, relay_h, relay_sem.at[2], relay_sem.at[1], diagonal)
 
     def relay_on(first):
         dst, k, where = (lo_h, 0, before) if first else (hi_h, 1, after)
-        return send(relay_h, dst.at[0, :, early], relay_sem.at[2], d_recv.at[k, 0], where)
+        return send(relay_h, dst.at[0, early, :], relay_sem.at[2], d_recv.at[k, 0], where)
 
     def late_copies():
         return (
-            send(od.at[:, late], lo_h.at[0, :, late], d_send.at[0, 0], d_recv.at[0, 0], after),
-            send(od.at[:, late], hi_h.at[0, :, late], d_send.at[1, 0], d_recv.at[1, 0], before),
+            send(od.at[late, cols(0)], lo_h.at[0, late, :], d_send.at[0, 0], d_recv.at[0, 0], after),
+            send(od.at[late, cols(0)], hi_h.at[0, late, :], d_send.at[1, 0], d_recv.at[1, 0], before),
         )
 
     def cross_out(first):
@@ -238,27 +239,45 @@
         dst, where = (ghi, before) if first else (glo, after)
         return send(summing, dst.at[rows_b, :], cross_sem.at[4], cross_sem.at[5], where)
 
-    def partial(d):
+    def head(i):
+        return cols(i, HEAD), i
+
+    def block(d):
+        return cols(d), d + COLS // HEAD - 1
+
+    n_heads = COLS // HEAD
+    last = n_cols + n_heads - 2
+
+    def partial(d, carry):
         part[:, cols(d)] = dot(hid[...], wd[:, cols(d)], ((1,), (0,))).astype(BF16)
-        p_copy(d).start()
-
-    def join(d):
-        p_copy(d).wait()
-        total = part[mine, cols(d)].astype(F32) + part_in[:, cols(d)].astype(F32)
-        part[mine, cols(d)] = total.astype(BF16)
-        q_copy(d).start()
-
-    partial(0)
-    partial(1)
-
-    def spread(i, carry):
-        join(i)
-        partial(i + 2)
-        return carry
-
-    lax.fori_loop(0, n_cols - 2, spread, 0)
-    join(n_cols - 2)
-    join(n_cols - 1)
+
+        @pl.when(d == 0)
+        def _():
+            for i in range(n_heads):
+                p_copy(*head(i)).start()
+
+        pl.when(d > 0)(p_copy(*block(d)).start)
+        return carry
+
+    def join(at, k):
+        p_copy(at, k).wait()
+        total = part[mine, at].astype(F32) + part_in[:, at].astype(F32)
+        part[mine, at] = total.astype(BF16)
+        q_copy(at, k).start()
+
+    def join_head(i, carry):
+        join(*head(i))
+        return carry
+
+    def spread(d, carry):
+        partial(d, carry)
+        join(*block(d - 1))
+        return carry
+
+    lax.fori_loop(0, 2, partial, 0)
+    lax.fori_loop(0, n_heads, join_head, 0)
+    lax.fori_loop(2, n_cols, spread, 0)
+    join(*block(n_cols - 1))
 
     def turn(i, carry):
         hid_t[cols(i), :] = hid[:, cols(i)].T
@@ -274,29 +293,41 @@
     lax.fori_loop(0, toks // 64, norm, 0)
     tgt_copy.wait()
 
-    def down(d, carry):
-        q_copy(d).wait()
-
-        @pl.when(jnp.logical_and(at_end, d == n_cols - 1))
+    def step_down(at, k):
+        q_copy(at, k).wait()
+
+        @pl.when(jnp.logical_and(at_end, k == last))
         def _():
             tell(go_sem, facing)
 
-        total = part[mine, cols(d)].astype(F32) + sum_in[:, cols(d)].astype(F32)
-        offset = x[mine, cols(d)].astype(F32) - tg[:, cols(d)].astype(F32)
-        err[mine, cols(d)] = ((offset + total * mid_scale) / toks).astype(BF16)
-        e_copy(d).start()
-        e_copy(d).wait()
-        grad = dot(hid_t[...], err[:, cols(d)], ((1,), (0,)))
-        od[:, cols(d)] = (
-            wd[:, cols(d)].astype(F32) - (step_size * mid_scale) * grad
-        ).astype(BF16)
-        ahead, behind = d_copies(d)
+        total = part[mine, at].astype(F32) + sum_in[:, at].astype(F32)
+        offset = x[mine, at].astype(F32) - tg[:, at].astype(F32)
+        err[mine, at] = ((offset + total * mid_scale) / toks).astype(BF16)
+        e_copy(at, k).start()
+        e_copy(at, k).wait()
+        grad = dot(hid_t[...], err[:, at], ((1,), (0,)))
+        od[:, at] = (wd[:, at].astype(F32) - (step_size * mid_scale) * grad).astype(BF16)
+
+    def inward_start(ahead, behind):
         pl.when(jnp.logical_not(last_end))(ahead.start)
         pl.when(jnp.logical_not(first_end))(behind.start)
-        pl.when(jnp.logical_and(at_end, d == 0))(relay_out().start)
-        return carry
-
-    lax.fori_loop(0, n_cols, down, 0)
+
+    def down_head(i, carry):
+        at, k = head(i)
+        step_down(at, k)
+        inward_start(
+            *pair(od.at[:, at], lo_h.at[0, :, at], hi_h.at[0, :, at], d_send, d_recv, 0)
+        )
+        return carry
+
+    def down(d, carry):
+        step_down(*block(d))
+        inward_start(*d_copies(d))
+        return carry
+
+    lax.fori_loop(0, n_heads, down_head, 0)
+    pl.when(at_end)(relay_out().start)
+    lax.fori_loop(1, n_cols, down, 0)
 
     @pl.when(at_end)
     def _():
@@ -500,7 +531,7 @@
             pltpu.VMEM((units, width), BF16),
             received,
             received,
-            jax.ShapeDtypeStruct((units, FIRST), BF16),
+            jax.ShapeDtypeStruct((FIRST, COLS), BF16),
         ),
         in_specs=[any_spec] * 5,
         out_specs=(vmem_spec, vmem_spec, vmem_spec, any_spec, any_spec, any_spec),
@@ -530,12 +561,12 @@
             dma((4,)),
             dma((2,)),
             dma((2, n_units)),
-            dma((n_cols,)),
-            dma((n_cols,)),
-            dma((n_cols,)),
-            dma((n_cols,)),
-            dma((n_cols,)),
-            dma((n_cols,)),
+            dma((n_cols + COLS // HEAD - 1,)),
+            dma((n_cols + COLS // HEAD - 1,)),
+            dma((n_cols + COLS // HEAD - 1,)),
+            dma((n_cols + COLS // HEAD - 1,)),
+            dma((n_cols + COLS // HEAD - 1,)),
+            dma((n_cols + COLS // HEAD - 1,)),
             dma((2, n_cols)),
             dma((2, n_cols)),
             dma((2, n_rest)),

time: 308 us -> 306 us (level)
  no operation moved by 1% of the time
where the time goes in v5:
time: 306 us
  Pallas kernels  305 us (100%)
    pallas_call x1, Pallas kernels, local(): pl.pallas_call(functools.partial(kernel, replicas), out_shape=(pltpu.VMEM...  301 us

profile of v5, /device:TPU:1, one launch (start us, length us, event | category | flops | bytes accessed | tf_op | source)
XLA Modules:
  0.0 305.9 jit_solution(16780592491667208021)
XLA Ops:
  0.6 300.6 %shard_map.76 = (bf16[2048,1024]{1,0:T(8,128)(2,1)S(1)}, bf16[2048,1024]{1,0:T(8,128)(2,1)S(1)}, bf16[1024,2048]{1,0:T(8,128)(2,1)S(1)}, bf16[8,1024,256]{2,1,0:...) custom-call(bf16[512,2048]{1,0:T(8,128)(2,1)} %bitcast.8, bf16[512,2048]{1,0:T(8,128)(2,1)} %bitcast.9, ...), custom_call_target="tpu_custom_call" | custom-call | tf_op jit(solution)/shard_map/pallas_call | solution.py:526
  301.3 4.7 %shard_map.77 = (bf16[1,2048,1024]{2,1,0:T(8,128)(2,1)}, bf16[1,2048,1024]{2,1,0:T(8,128)(2,1)}, bf16[1,1024,2048]{2,1,0:T(8,128)(2,1)}) custom-call(bf16[2048,1024]{1,0:T(8,128)(2,1)S(1)} %get-tuple-element.6.refs_0_, bf16[2048,1024]{1,0:T(8,128)(2,1)S(1)} %get-tuple-element.7.refs_1_, bf16[1024,2048]{1,0:T(8,128)(2,1)S(1)} %get-tuple-element.8.refs_2_), custom_call_target="tpu_custom_call" | custom-call | tf_op jit(solution)/shard_map/pallas_call | solution.py:506

commit v6 on v5

--- a/solution.py
+++ b/solution.py
@@ -13,9 +13,10 @@
 COLS = 256
 X, Y = 4, 2
 ROWS = 256
-REST = 368
-AWAY = 208
-FIRST = 768
+REST = 272
+AWAY = 144
+FIRST = 512
+DETOUR = 2
 HEAD = 128
 
 
@@ -26,12 +27,12 @@
 def kernel(
     replicas,
     tok_h, tgt_h, wg_h, wu_h, wd_h,
-    og, ou, od, lo_h, hi_h, relay_h,
+    og, ou, od, lo_h, hi_h,
     x, tg, inv, nrm, wd, slope, act, hid, hid_t, err, gg, gu,
-    part, part_in, sum_in, glo, ghi, ulo, uhi, stage, crossing, summing,
+    part, part_in, sum_in, passing, glo, ghi, ulo, uhi, stage, crossing, summing, relayed,
     tok_sem, load_sem, w_sem, p_send, p_recv, q_send, q_recv, e_send, e_recv,
     d_send, d_recv, g_send, g_recv, u_send, u_recv, st_sem,
-    b_send, b_recv, relay_sem, cross_sem, go_sem,
+    b_send, b_recv, relay_sem, cross_sem, pass_sem, go_sem,
 ):
     g = lax.axis_index("gossip")
     m = lax.axis_index("mp")
@@ -103,7 +104,8 @@
     diagonal = lax.rem(g + (X + 1) * (1 - 2 * lax.rem(along, 2)) + replicas, replicas)
     across_up = lax.rem(g + X, replicas)
     across_down = lax.rem(g - X + replicas, replicas)
-    near = ((g, sibling), (g, peer), (diagonal, m))
+    beside = g + 1 - 2 * lax.rem(along, 2)
+    near = ((g, sibling), (g, peer), (diagonal, m), (beside, peer))
     inward = g + 1 - 2 * (along // (X - 1))
 
     @pl.when(jnp.logical_not(at_end))
@@ -151,6 +153,16 @@
     def _():
         pl.semaphore_wait(barrier, len(near) + 1 + len(facing))
 
+    def head(i):
+        return cols(i, HEAD), i
+
+    def block(d):
+        return cols(d), d + COLS // HEAD - 1
+
+    n_heads = COLS // HEAD
+    last = n_cols + n_heads - 2 - DETOUR
+    inside = jnp.logical_not(at_end)
+
     def p_copy(at, k):
         return pltpu.make_async_remote_copy(
             src_ref=part.at[theirs, at], dst_ref=part_in.at[:, at],
@@ -163,6 +175,22 @@
             src_ref=part.at[mine, at], dst_ref=sum_in.at[:, at],
             send_sem=q_send.at[k], recv_sem=q_recv.at[k],
             device_id=(g, peer), device_id_type=MESH,
+        )
+
+    def detour_out(i):
+        d = n_cols - DETOUR + i
+        return pltpu.make_async_remote_copy(
+            src_ref=part.at[mine, cols(d)], dst_ref=passing.at[i],
+            send_sem=q_send.at[block(d)[1]], recv_sem=pass_sem.at[0, i],
+            device_id=(beside, peer), device_id_type=MESH,
+        )
+
+    def detour_on(i):
+        d = n_cols - DETOUR + i
+        return pltpu.make_async_remote_copy(
+            src_ref=passing.at[i], dst_ref=sum_in.at[:, cols(d)],
+            send_sem=pass_sem.at[1, i], recv_sem=q_recv.at[block(d)[1]],
+            device_id=(beside, m), device_id_type=MESH,
         )
 
     def e_copy(at, k):
@@ -213,19 +241,19 @@
         )
 
     def relay_out():
-        return send(od.at[early, cols(0)], relay_h, relay_sem.at[0], relay_sem.at[1], far_end)
+        return send(od.at[early, cols(1)], relayed, relay_sem.at[0], relay_sem.at[1], far_end)
 
     def relay_over():
-        return send(relay_h, relay_h, relay_sem.at[2], relay_sem.at[1], diagonal)
+        return send(relayed, relayed, relay_sem.at[2], relay_sem.at[1], diagonal)
 
     def relay_on(first):
         dst, k, where = (lo_h, 0, before) if first else (hi_h, 1, after)
-        return send(relay_h, dst.at[0, early, :], relay_sem.at[2], d_recv.at[k, 0], where)
+        return send(relayed, dst.at[1, early, :], relay_sem.at[2], d_recv.at[k, 1], where)
 
     def late_copies():
         return (
-            send(od.at[late, cols(0)], lo_h.at[0, late, :], d_send.at[0, 0], d_recv.at[0, 0], after),
-            send(od.at[late, cols(0)], hi_h.at[0, late, :], d_send.at[1, 0], d_recv.at[1, 0], before),
+            send(od.at[late, cols(1)], lo_h.at[1, late, :], d_send.at[0, 1], d_recv.at[0, 1], after),
+            send(od.at[late, cols(1)], hi_h.at[1, late, :], d_send.at[1, 1], d_recv.at[1, 1], before),
         )
 
     def cross_out(first):
@@ -238,15 +266,6 @@
     def cross_end(first):
         dst, where = (ghi, before) if first else (glo, after)
         return send(summing, dst.at[rows_b, :], cross_sem.at[4], cross_sem.at[5], where)
-
-    def head(i):
-        return cols(i, HEAD), i
-
-    def block(d):
-        return cols(d), d + COLS // HEAD - 1
-
-    n_heads = COLS // HEAD
-    last = n_cols + n_heads - 2
 
     def partial(d, carry):
         part[:, cols(d)] = dot(hid[...], wd[:, cols(d)], ((1,), (0,))).astype(BF16)
@@ -263,7 +282,9 @@
         p_copy(at, k).wait()
         total = part[mine, at].astype(F32) + part_in[:, at].astype(F32)
         part[mine, at] = total.astype(BF16)
-        q_copy(at, k).start()
+        straight = jnp.logical_or(k <= last, inside)
+        pl.when(straight)(q_copy(at, k).start)
+        pl.when(jnp.logical_not(straight))(detour_out(jnp.maximum(k - last - 1, 0)).start)
 
     def join_head(i, carry):
         join(*head(i))
@@ -290,7 +311,6 @@
         nrm[rows, :] = (x[rows, :].astype(F32) * inv[rows, :]).astype(BF16)
         return carry
 
-    lax.fori_loop(0, toks // 64, norm, 0)
     tgt_copy.wait()
 
     def step_down(at, k):
@@ -321,13 +341,39 @@
         return carry
 
     def down(d, carry):
+        @pl.when(jnp.logical_and(inside, d <= DETOUR))
+        def _():
+            i = jnp.minimum(d, DETOUR) - 1
+            detour_out(i).wait_recv()
+            detour_on(i).start()
+
         step_down(*block(d))
-        inward_start(*d_copies(d))
+
+        @pl.when(d != 1)
+        def _():
+            inward_start(*d_copies(d))
+
+        @pl.when(d == 1)
+        def _():
+            ahead, behind = d_copies(1)
+            late_ahead, late_behind = late_copies()
+            pl.when(along <= 1)(ahead.start)
+            pl.when(along >= 2)(behind.start)
+            pl.when(along == 2)(late_ahead.start)
+            pl.when(along == 1)(late_behind.start)
+            pl.when(at_end)(relay_out().start)
+
+        return carry
+
+    def down_late(d, carry):
+        step_down(*block(d))
+        for copy in d_copies(d):
+            copy.start()
         return carry
 
     lax.fori_loop(0, n_heads, down_head, 0)
-    pl.when(at_end)(relay_out().start)
-    lax.fori_loop(1, n_cols, down, 0)
+    lax.fori_loop(0, toks // 64, norm, 0)
+    lax.fori_loop(1, n_cols - DETOUR, down, 0)
 
     @pl.when(at_end)
     def _():
@@ -339,10 +385,12 @@
         pl.when(first_end)(behind.start)
         return carry
 
+    held_back(0, 0)
     ahead, behind = late_copies()
     pl.when(last_end)(ahead.start)
     pl.when(first_end)(behind.start)
-    lax.fori_loop(1, n_cols, held_back, 0)
+    lax.fori_loop(2, n_cols - DETOUR, held_back, 0)
+    lax.fori_loop(n_cols - DETOUR, n_cols, down_late, 0)
 
     def back(f, carry):
         grad = dot(err[...], wd[cols(f), :], ((1,), (1,))) * mid_scale
@@ -371,7 +419,6 @@
         return carry
 
     lower, upper = along <= 1, along >= 2
-    inside = jnp.logical_not(at_end)
     first_in, last_in = along == 1, along == 2
 
     def step_gate(i, carry):
@@ -394,15 +441,8 @@
         return ((lo.astype(F32) + own.astype(F32) + hi.astype(F32)) / 3.0).astype(BF16)
 
     def mix_down(d, carry):
-        ahead, behind = d_copies(d)
-        ahead.wait_recv()
-        behind.wait_recv()
-        pl.when(jnp.logical_not(jnp.logical_and(last_end, d == 0)))(ahead.wait_send)
-        pl.when(jnp.logical_not(jnp.logical_and(first_end, d == 0)))(behind.wait_send)
-        ahead, behind = late_copies()
-        pl.when(jnp.logical_and(last_end, d == 0))(ahead.wait_send)
-        pl.when(jnp.logical_and(first_end, d == 0))(behind.wait_send)
-        pl.when(jnp.logical_and(at_end, d == 0))(relay_out().wait_send)
+        for copy in d_copies(d):
+            copy.wait()
         loads = [
             pltpu.make_async_copy(lo_h.at[d], stage.at[0], st_sem.at[0]),
             pltpu.make_async_copy(hi_h.at[d], stage.at[1], st_sem.at[1]),
@@ -414,11 +454,14 @@
         od[:, cols(d)] = third(stage[0], od[:, cols(d)], stage[1])
         return carry
 
-    lax.fori_loop(1, n_cols, mix_down, 0)
+    mix_down(0, 0)
+    lax.fori_loop(2, n_cols, mix_down, 0)
 
     @pl.when(inside)
     def _():
         relay_out().wait_recv()
+        both = relayed[...].astype(F32) + od[early, cols(1)].astype(F32)
+        relayed[...] = both.astype(BF16)
         pl.when(first_in)(relay_on(True).start)
         pl.when(last_in)(relay_on(False).start)
         for copy in b_copies():
@@ -441,7 +484,53 @@
         return carry
 
     lax.fori_loop(0, n_rest, mix_gate, 0)
-    lax.fori_loop(0, 1, mix_down, 0)
+    ahead, behind = d_copies(1)
+    late_ahead, late_behind = late_copies()
+    pl.when(lower)(ahead.wait_send)
+    pl.when(upper)(behind.wait_send)
+    pl.when(upper)(late_ahead.wait_send)
+    pl.when(lower)(late_behind.wait_send)
+    pl.when(at_end)(relay_out().wait_send)
+    pl.when(jnp.logical_not(last_end))(ahead.wait_recv)
+    pl.when(jnp.logical_not(first_end))(behind.wait_recv)
+    pl.when(last_end)(late_ahead.wait_recv)
+    pl.when(first_end)(late_behind.wait_recv)
+
+    def load_second(rows, k):
+        held = hi_h if k else lo_h
+        return pltpu.make_async_copy(held.at[1, rows, :], stage.at[k, rows, :], st_sem.at[k])
+
+    def third_second(rows):
+        loads = [load_second(rows, k) for k in range(2)]
+        for load in loads:
+            load.start()
+        for load in loads:
+            load.wait()
+        od[rows, cols(1)] = third(stage[0, rows, :], od[rows, cols(1)], stage[1, rows, :])
+
+    third_second(late)
+
+    @pl.when(inside)
+    def _():
+        third_second(early)
+
+    def end(own, both):
+        return ((own.astype(F32) + both.astype(F32)) / 3.0).astype(BF16)
+
+    def end_second(k):
+        load = load_second(early, k)
+        load.start()
+        load.wait()
+        od[early, cols(1)] = end(od[early, cols(1)], stage[k, early, :])
+
+    @pl.when(first_end)
+    def _():
+        end_second(0)
+
+    @pl.when(last_end)
+    def _():
+        end_second(1)
+
     ahead, behind = b_copies()
     pl.when(lower)(ahead.wait_send)
     pl.when(upper)(behind.wait_send)
@@ -464,10 +553,12 @@
 
     lax.fori_loop(0, n_rows, mix_up, 0)
 
-    def end(own, both):
-        return ((own.astype(F32) + both.astype(F32)) / 3.0).astype(BF16)
-
     relay_over().wait_send()
+
+    @pl.when(inside)
+    def _():
+        for i in range(DETOUR):
+            detour_on(i).wait_send()
 
     @pl.when(inside)
     def _():
@@ -531,10 +622,9 @@
             pltpu.VMEM((units, width), BF16),
             received,
             received,
-            jax.ShapeDtypeStruct((FIRST, COLS), BF16),
         ),
         in_specs=[any_spec] * 5,
-        out_specs=(vmem_spec, vmem_spec, vmem_spec, any_spec, any_spec, any_spec),
+        out_specs=(vmem_spec, vmem_spec, vmem_spec, any_spec, any_spec),
         scratch_shapes=[
             pltpu.VMEM((toks, width), BF16),
             pltpu.VMEM((half, width), BF16),
@@ -551,6 +641,7 @@
             pltpu.VMEM((toks, width), BF16),
             pltpu.VMEM((half, width), BF16),
             pltpu.VMEM((half, width), BF16),
+            pltpu.VMEM((DETOUR, half, COLS), BF16),
             pltpu.VMEM((width, units), BF16),
             pltpu.VMEM((width, units), BF16),
             pltpu.VMEM((width, units), BF16),
@@ -558,6 +649,7 @@
             pltpu.VMEM((2, units, COLS), BF16),
             pltpu.VMEM((AWAY, units), BF16),
             pltpu.VMEM((AWAY, units), BF16),
+            pltpu.VMEM((FIRST, COLS), BF16),
             dma((4,)),
             dma((2,)),
             dma((2, n_units)),
@@ -578,6 +670,7 @@
             dma((2,)),
             dma((3,)),
             dma((6,)),
+            dma((2, DETOUR)),
             pltpu.SemaphoreType.REGULAR,
         ],
         compiler_params=pltpu.CompilerParams(

time: 306 us -> 306 us (level)
  no operation moved by 1% of the time
where the time goes in v6:
time: 306 us
  Pallas kernels  305 us (100%)
    pallas_call x1, Pallas kernels, local(): pl.pallas_call(functools.partial(kernel, replicas), out_shape=(pltpu.VMEM...  300 us

profile of v6, /device:TPU:1, one launch (start us, length us, event | category | flops | bytes accessed | tf_op | source)
XLA Modules:
  0.0 305.5 jit_solution(16292946082353153519)
XLA Ops:
  0.6 300.2 %shard_map.76 = (bf16[2048,1024]{1,0:T(8,128)(2,1)S(1)}, bf16[2048,1024]{1,0:T(8,128)(2,1)S(1)}, bf16[1024,2048]{1,0:T(8,128)(2,1)S(1)}, bf16[8,1024,256]{2,1,0:T(8,128)(2,1)}, bf16[8,1024,256]{2,1,0:T(8,128)(2,1)}) custom-call(bf16[512,2048]{1,0:T(8,128)(2,1)} %bitcast.8, bf16[512,2048]{1,0:T(8,128)(2,1)} %bitcast.9, bf16[2048,1024]{1,0:T(8,128)(2,1)} %bitcast.5, ...), custom_call_target="tpu_custom_call" | custom-call | tf_op jit(solution)/shard_map/pallas_call | solution.py:617
  300.8 4.7 %shard_map.77 = (bf16[1,2048,1024]{2,1,0:T(8,128)(2,1)}, bf16[1,2048,1024]{2,1,0:T(8,128)(2,1)}, bf16[1,1024,2048]{2,1,0:T(8,128)(2,1)}) custom-call(bf16[2048,1024]{1,0:T(8,128)(2,1)S(1)} %get-tuple-element.6.refs_0_, bf16[2048,1024]{1,0:T(8,128)(2,1)S(1)} %get-tuple-element.7.refs_1_, bf16[1024,2048]{1,0:T(8,128)(2,1)S(1)} %get-tuple-element.8.refs_2_), custom_call_target="tpu_custom_call" | custom-call | tf_op jit(solution)/shard_map/pallas_call | solution.py:597

commit v7 on v6

--- a/solution.py
+++ b/solution.py
@@ -13,9 +13,9 @@
 COLS = 256
 X, Y = 4, 2
 ROWS = 256
-REST = 272
-AWAY = 144
-FIRST = 512
+REST = 208
+AWAY = 176
+FIRST = 448
 DETOUR = 2
 HEAD = 128
 

time: 306 us -> 305 us (level)
  no operation moved by 1% of the time
where the time goes in v7:
time: 305 us
  Pallas kernels  304 us (100%)
    pallas_call x1, Pallas kernels, local(): pl.pallas_call(functools.partial(kernel, replicas), out_shape=(pltpu.VMEM...  300 us

profile of v7, /device:TPU:1, one launch (start us, length us, event | category | flops | bytes accessed | tf_op | source)
XLA Modules:
  0.0 304.9 jit_solution(321838095931910482)
XLA Ops:
  0.6 299.6 %shard_map.76 = (bf16[2048,1024]{1,0:T(8,128)(2,1)S(1)}, bf16[2048,1024]{1,0:T(8,128)(2,1)S(1)}, bf16[1024,2048]{1,0:T(8,128)(2,1)S(1)}, bf16[8,1024,256]{2,1,0:T(8,128)(2,1)}, bf16[8,1024,256]{2,1,0:T(8,128)(2,1)}) custom-call(bf16[512,2048]{1,0:T(8,128)(2,1)} %bitcast.8, bf16[512,2048]{1,0:T(8,128)(2,1)} %bitcast.9, bf16[2048,1024]{1,0:T(8,128)(2,1)} %bitcast.5, ...), custom_call_target="tpu_custom_call" | custom-call | tf_op jit(solution)/shard_map/pallas_call | solution.py:617
  300.2 4.7 %shard_map.77 = (bf16[1,2048,1024]{2,1,0:T(8,128)(2,1)}, bf16[1,2048,1024]{2,1,0:T(8,128)(2,1)}, bf16[1,1024,2048]{2,1,0:T(8,128)(2,1)}) custom-call(bf16[2048,1024]{1,0:T(8,128)(2,1)S(1)} %get-tuple-element.6.refs_0_, bf16[2048,1024]{1,0:T(8,128)(2,1)S(1)} %get-tuple-element.7.refs_1_, bf16[1024,2048]{1,0:T(8,128)(2,1)S(1)} %get-tuple-element.8.refs_2_), custom_call_target="tpu_custom_call" | custom-call | tf_op jit(solution)/shard_map/pallas_call | solution.py:597

commit v8 on v7

--- a/solution.py
+++ b/solution.py
@@ -341,9 +341,9 @@
         return carry
 
     def down(d, carry):
-        @pl.when(jnp.logical_and(inside, d <= DETOUR))
+        @pl.when(jnp.logical_and(inside, jnp.logical_and(d >= 2, d < 2 + DETOUR)))
         def _():
-            i = jnp.minimum(d, DETOUR) - 1
+            i = lax.rem(d + DETOUR - 2, DETOUR)
             detour_out(i).wait_recv()
             detour_on(i).start()
 

time: 305 us -> 305 us (level)
  no operation moved by 1% of the time
where the time goes in v8:
time: 305 us
  Pallas kernels  304 us (100%)
    pallas_call x1, Pallas kernels, local(): pl.pallas_call(functools.partial(kernel, replicas), out_shape=(pltpu.VMEM...  300 us

profile of v8, /device:TPU:1, one launch (start us, length us, event | category | flops | bytes accessed | tf_op | source)
XLA Modules:
  0.0 304.9 jit_solution(14357939500409734955)
XLA Ops:
  0.6 299.6 %shard_map.76 = (bf16[2048,1024]{1,0:T(8,128)(2,1)S(1)}, bf16[2048,1024]{1,0:T(8,128)(2,1)S(1)}, bf16[1024,2048]{1,0:T(8,128)(2,1)S(1)}, bf16[8,1024,256]{2,1,0:T(8,128)(2,1)}, bf16[8,1024,256]{2,1,0:T(8,128)(2,1)}) custom-call(bf16[512,2048]{1,0:T(8,128)(2,1)} %bitcast.8, bf16[512,2048]{1,0:T(8,128)(2,1)} %bitcast.9, bf16[2048,1024]{1,0:T(8,128)(2,1)} %bitcast.5, ...), custom_call_target="tpu_custom_call" | custom-call | tf_op jit(solution)/shard_map/pallas_call | solution.py:617
  300.2 4.7 %shard_map.77 = (bf16[1,2048,1024]{2,1,0:T(8,128)(2,1)}, bf16[1,2048,1024]{2,1,0:T(8,128)(2,1)}, bf16[1,1024,2048]{2,1,0:T(8,128)(2,1)}) custom-call(bf16[2048,1024]{1,0:T(8,128)(2,1)S(1)} %get-tuple-element.6.refs_0_, bf16[2048,1024]{1,0:T(8,128)(2,1)S(1)} %get-tuple-element.7.refs_1_, bf16[1024,2048]{1,0:T(8,128)(2,1)S(1)} %get-tuple-element.8.refs_2_), custom_call_target="tpu_custom_call" | custom-call | tf_op jit(solution)/shard_map/pallas_call | solution.py:597

commit v9 on v7

--- a/solution.py
+++ b/solution.py
@@ -372,7 +372,6 @@
         return carry
 
     lax.fori_loop(0, n_heads, down_head, 0)
-    lax.fori_loop(0, toks // 64, norm, 0)
     lax.fori_loop(1, n_cols - DETOUR, down, 0)
 
     @pl.when(at_end)
@@ -404,6 +403,8 @@
     def _():
         relay_out().wait_recv()
         relay_over().start()
+
+    lax.fori_loop(0, toks // 64, norm, 0)
 
     def step(out, grads, rows):
         grad = dot(nrm[:, rows], grads[...], ((0,), (0,)))

time: 305 us -> 305 us (level)
  no operation moved by 1% of the time
where the time goes in v9:
time: 305 us
  Pallas kernels  304 us (100%)
    pallas_call x1, Pallas kernels, local(): pl.pallas_call(functools.partial(kernel, replicas), out_shape=(pltpu.VMEM...  300 us

profile of v9, /device:TPU:1, one launch (start us, length us, event | category | flops | bytes accessed | tf_op | source)
XLA Modules:
  0.0 304.9 jit_solution(15930719415331758747)
XLA Ops:
  0.6 299.6 %shard_map.76 = (bf16[2048,1024]{1,0:T(8,128)(2,1)S(1)}, bf16[2048,1024]{1,0:T(8,128)(2,1)S(1)}, bf16[1024,2048]{1,0:T(8,128)(2,1)S(1)}, bf16[8,1024,256]{2,1,0:T(8,128)(2,1)}, bf16[8,1024,256]{2,1,0:T(8,128)(2,1)}) custom-call(bf16[512,2048]{1,0:T(8,128)(2,1)} %bitcast.8, bf16[512,2048]{1,0:T(8,128)(2,1)} %bitcast.9, bf16[2048,1024]{1,0:T(8,128)(2,1)} %bitcast.5, ...), custom_call_target="tpu_custom_call" | custom-call | tf_op jit(solution)/shard_map/pallas_call | solution.py:618
  300.2 4.7 %shard_map.77 = (bf16[1,2048,1024]{2,1,0:T(8,128)(2,1)}, bf16[1,2048,1024]{2,1,0:T(8,128)(2,1)}, bf16[1,1024,2048]{2,1,0:T(8,128)(2,1)}) custom-call(bf16[2048,1024]{1,0:T(8,128)(2,1)S(1)} %get-tuple-element.6.refs_0_, bf16[2048,1024]{1,0:T(8,128)(2,1)S(1)} %get-tuple-element.7.refs_1_, bf16[1024,2048]{1,0:T(8,128)(2,1)S(1)} %get-tuple-element.8.refs_2_), custom_call_target="tpu_custom_call" | custom-call | tf_op jit(solution)/shard_map/pallas_call | solution.py:598
